TPU v7x, 256 devices: a 4x2x16 block of a 4x16x16 slice. The times are simulated.
256 devices in a mesh: grp: 2 (over y), seq: 128 (over z, x, core).
Axes of the slice: x: 4, y: 2, z: 16, core: 2. Of those that a mesh axis runs over, the one named last changes fastest.
The devices are a block of a 4x16x16 slice.
Arguments:
- frames: bfloat16 [4, 81920, 1280], P('grp', 'seq'), parts along dimension 0, may hold values from -120 to 120
- dec_states: bfloat16 [2, 256, 1280], P(None, 'grp'), parts along dimension 1, may hold values from -6 to 6
- w_query: bfloat16 [1280, 1280], P(None, 'seq'), may hold values from -0.15625 to 0.15625
- w_keyval: bfloat16 [1280, 2560], replicated, may hold values from -0.15625 to 0.15625
- w_output: bfloat16 [1280, 1280], P(None, 'seq'), may hold values from -0.15625 to 0.15625
- head_slope: float32 [20], replicated, may hold values from 0.3 to 12
- lengths: int32 [4, 128], P('grp'), parts along dimension 0, may hold values from 128 to 640, as said below
- positions: int32 [2, 256], P(None, 'grp'), parts along dimension 1, may hold values from 0 to 127
Outputs:
- attended: bfloat16 [2, 256, 1280], P(None, 'grp', 'seq'), parts along dimension 1
There are 2 independent parts, one for each index of `grp`. A program takes and returns all parts, laid end to end along the dimension named above; an argument that names none is the same for every part. Nothing has to cross between parts.
Inputs may be any that keep to these rules, and one draw needn't show every extreme that they name: `lengths`: every step has one block of exactly 640 valid frames.
All inputs are finite; a program needn't handle non-finite values.
Results may differ from a plain program's by a relative error of at most 0.005.
The roundings to bfloat16 on the way count: a program that leaves them out, or rounds other values in their place, can miss the bound.
Values may be sent and summed in bfloat16 or wider, within the bound.
A program may use at most 128 MiB of HBM per device.

v0:
```python
import functools
import math

import jax
import jax.numpy as jnp
from jax import lax
from jax.sharding import Mesh
from jax.sharding import PartitionSpec as P

SEQ = ("seq_0", "seq_1", "seq_2")


def in_order(tiles, dim):
    tiles = jnp.moveaxis(tiles, 0, dim)
    dims = tiles.shape
    return tiles.reshape(*dims[:dim], dims[dim] * dims[dim + 1], *dims[dim + 2 :])


def all_blocks(x, axes, sequence):
    tiles = x
    for k in sequence:
        tiles = lax.all_gather(tiles, axes[k])
    done = sequence[::-1]
    back = [done.index(k) for k in range(len(axes))]
    tiles = tiles.transpose(*back, *range(len(axes), tiles.ndim))
    return tiles.reshape(-1, *x.shape)


def gathered_by_axis(x, axes, sequence, dim):
    return in_order(all_blocks(x, axes, sequence), dim)


def combined_by_axis(x, axes, combine):
    for axis in axes:
        pieces = jax.tree.map(lambda part: lax.all_gather(part, axis), x)
        x = jax.tree.map(lambda part: part[0], pieces)
        for k in range(1, lax.axis_size(axis)):
            x = combine(x, jax.tree.map(lambda part: part[k], pieces))
    return x


def block_partial(
    queries,
    block_keys,
    block_values,
    length_now,
    slot_place,
    age_steps,
    row_positions,
    head_slope,
    devices,
):
    query_rows, head_count, head_size = queries.shape
    frame_count = block_keys.shape[0]
    keys_split = block_keys.reshape(frame_count, head_count, head_size)
    scores = jnp.einsum(
        "qhd,jhd->hqj", queries, keys_split, preferred_element_type=jnp.float32
    ) / math.sqrt(head_size)
    distance = (
        jnp.abs(row_positions.astype(jnp.float32) - slot_place.astype(jnp.float32)) / devices
        + age_steps
    )
    scores = scores - head_slope[:, None, None] * distance[None, :, None]
    valid = lax.broadcasted_iota(jnp.int32, (1, 1, frame_count), 2) < length_now
    scores = jnp.where(valid, scores, -jnp.inf)
    row_peak = jnp.max(scores, axis=2)
    weights = jnp.exp(scores - row_peak[:, :, None]).astype(jnp.bfloat16)
    row_total = jnp.sum(weights.astype(jnp.float32), axis=2)
    values_split = block_values.reshape(frame_count, head_count, head_size)
    row_context = jnp.einsum(
        "hqj,jhd->qhd", weights, values_split, preferred_element_type=jnp.float32
    )
    return (row_peak.T, row_total.T, row_context.reshape(query_rows, head_count * head_size))


def rescale(row_context, factors, head_count):
    query_rows = row_context.shape[0]
    spread_rows = row_context.reshape(query_rows, head_count, -1) * factors[:, :, None]
    return spread_rows.reshape(query_rows, -1)


def combine_parts(head_count, earlier, later):
    peak_one, total_one, context_one = earlier
    peak_two, total_two, context_two = later
    row_top = jnp.maximum(peak_one, peak_two)
    scale_one = jnp.exp(peak_one - row_top)
    scale_two = jnp.exp(peak_two - row_top)
    merged_total = total_one * scale_one + total_two * scale_two
    merged_context = rescale(context_one, scale_one, head_count) + rescale(
        context_two, scale_two, head_count
    )
    return (row_top, merged_total, merged_context)


def local(frames, dec_states, w_query, w_keyval, w_output, head_slope, lengths, positions):
    devices = lax.axis_size(SEQ)
    own_index = lax.axis_index(SEQ)
    step_count, frame_count, model_width = frames.shape
    query_rows = dec_states.shape[1]
    head_count = head_slope.shape[0]
    head_size = model_width // head_count
    frame_rows = frames.reshape(step_count * frame_count, model_width)
    keyval = jnp.dot(frame_rows, w_keyval, preferred_element_type=jnp.float32).astype(jnp.bfloat16)
    block_keys = keyval[:, :model_width].reshape(step_count, frame_count, model_width)
    block_values = keyval[:, model_width:].reshape(step_count, frame_count, model_width)
    dec_rows = dec_states.reshape(step_count * query_rows, model_width)
    local_query = jnp.dot(dec_rows, w_query, preferred_element_type=jnp.float32).astype(
        jnp.bfloat16
    )
    queries = gathered_by_axis(local_query, SEQ, (0, 1, 2), 1)
    queries = queries.reshape(step_count, query_rows, head_count, head_size)
    combine = functools.partial(combine_parts, head_count)
    slot_place = (own_index + 1) % devices
    results = []
    for step_now in range(step_count):
        running = None
        for older_step in range(step_now + 1):
            partial_now = block_partial(
                queries[step_now],
                block_keys[older_step],
                block_values[older_step],
                lengths[older_step, own_index],
                slot_place,
                float(step_now - older_step),
                positions[step_now],
                head_slope,
                devices,
            )
            running = partial_now if running is None else combine(running, partial_now)
        row_peak, row_total, row_context = running
        row_top, row_total, row_context = combined_by_axis(
            (row_peak, row_total, row_context), SEQ, combine
        )
        context = row_context.reshape(query_rows, head_count, head_size) / row_total[:, :, None]
        context = context.reshape(query_rows, model_width).astype(jnp.bfloat16)
        results.append(
            jnp.dot(context, w_output, preferred_element_type=jnp.float32).astype(jnp.bfloat16)
        )
    return jnp.stack(results)


def solution(mesh):
    finer = Mesh(
        mesh.devices.reshape(mesh.shape["grp"], 16, 4, 2), ("grp", "seq_0", "seq_1", "seq_2")
    )
    return jax.shard_map(
        local,
        mesh=finer,
        in_specs=(
            P("grp", SEQ, None),
            P(None, "grp", None),
            P(None, SEQ),
            P(),
            P(None, SEQ),
            P(),
            P("grp", None),
            P(None, "grp"),
        ),
        out_specs=P(None, "grp", SEQ),
        check_vma=False,
    )
```

profile of v0, /device:TPU:33, one launch (start us, length us, event | category | flops | bytes accessed | tf_op | source)
XLA Modules:
  0.0 570.3 jit_solution(2481648747681104679)
XLA Ops:
  8.5 10.8 %convolution_convert_fusion = bf16[1280,2560]{1,0:T(8,128)(2,1)S(1)} fusion(bf16[1280,1280]{1,0:T(8,128)(2,1)S(1)} %bitcast.1433, bf16[1280,2560]{1,0:T(8,128)(2,1)} %param.11), kind=kOutput, calls=%fused_computation | convolution fusion | flops 8391884800 | bytes 16384000 | tf_op jit(solution)/shard_map/dot_general | solution.py:103
  21.5 3.5 copy.157
  27.6 42.8 %all-gather = bf16[4096,10]{0,1:T(8,128)(2,1)S(1)} all-gather(bf16[256,10]{0,1:T(8,128)(2,1)S(1)} %convolution_convert_fusion.1), channel_id=2, replica_groups=mesh['grp'=2,'seq_0'=16,'seq_1'=4,'seq_2'=2] {'seq_0'}, dimensions={0}, use_global_device_ids=true | all-gather | bytes 87040 | tf_op jit(solution)/shard_map/all_gather | solution.py:22
  70.4 10.2 %all-gather.1 = bf16[64,256,10]{1,0,2:T(8,128)(2,1)S(1)} all-gather(bf16[16,256,10]{1,0,2:T(8,128)(2,1)S(1)} %slice_bitcast_fusion), channel_id=3, replica_groups=mesh['grp'=2,'seq_0'=16,'seq_1'=4,'seq_2'=2] {'seq_1'}, dimensions={0}, use_global_device_ids=true | all-gather | bytes 409600 | tf_op jit(solution)/shard_map/all_gather | solution.py:22
  80.6 12.7 %all-gather.2 = bf16[8,16,256,10]{2,1,0,3:T(8,128)(2,1)S(1)} all-gather(bf16[4,16,256,10]{2,1,0,3:T(8,128)(2,1)S(1)} %bitcast.1442), channel_id=4, replica_groups=mesh['grp'=2,'seq_0'=16,'seq_1'=4,'seq_2'=2] {'seq_2'}, dimensions={0}, use_global_device_ids=true | all-gather | bytes 983040 | tf_op jit(solution)/shard_map/all_gather | solution.py:22
  94.8 2.7 reshape.3589
  102.4 3.5 copy.156
  106.6 2.2 copy.129
  112.2 2.7 fusion.274
  118.6 2.8 fusion
  121.5 4.3 convert_reduce_fusion.2
  131.6 4.1 fusion.259
  136.9 24.8 %all-gather.5 = f32[2048,20]{0,1:T(8,128)S(1)} all-gather(f32[128,20]{0,1:T(8,128)S(1)} %get-tuple-element.190), channel_id=7, replica_groups=mesh['grp'=2,'seq_0'=16,'seq_1'=4,'seq_2'=2] {'seq_0'}, dimensions={0}, use_global_device_ids=true | all-gather | bytes 174080 | tf_op jit(solution)/shard_map/all_gather | solution.py:35
  166.2 84.3 %all-gather.20.cloned.1.call-done = f32[16,128,1280]{2,1,0:T(8,128)} async-done(((f32[1,128,1280]{2,1,0:T(8,128)}), f32[16,128,1280]{2,1,0:T(8,128)}) %all-gather.20.cloned.1.call-update) | async-done | bytes 10485776 | tf_op jit(solution)/shard_map/all_gather | solution.py:35
  250.5 7.2 %fusion.267 = (f32[1,128,1280]{2,1,0:T(8,128)}, f32[1,128,1280]{2,1,0:T(8,128)S(1)}, f32[1,128,1280]{2,1,0:T(8,128)S(1)}, f32[1,128,1280]{2,1,0:T(8,128)S(1)}, f...) fusion(f32[16,128,1280]{2,1,0:T(8,128)} %all-gather.20.cloned.1, ...), kind=kLoop, calls=%fused_computation.595 | loop fusion | bytes 20971520 | tf_op jit(solution)/shard_map/slice | solution.py:36
  264.3 2.2 copy.215
  284.0 5.1 fusion.13
  291.4 27.5 %all-gather.3 = f32[2048,20]{0,1:T(8,128)S(1)} all-gather(f32[128,20]{0,1:T(8,128)S(1)} %bitcast.1449), channel_id=5, replica_groups=mesh['grp'=2,'seq_0'=16,'seq_1'=4,'seq_2'=2] {'seq_0'}, dimensions={0}, use_global_device_ids=true | all-gather | bytes 174080 | tf_op jit(solution)/shard_map/all_gather | solution.py:35
  323.4 53.6 %all-gather.14.cloned.1.call-done = f32[16,128,1280]{2,1,0:T(8,128)} async-done(((f32[1,128,1280]{2,1,0:T(8,128)}), f32[16,128,1280]{2,1,0:T(8,128)}) %all-gather.14.cloned.1.call-update) | async-done | bytes 10485776 | tf_op jit(solution)/shard_map/all_gather | solution.py:35
  377.0 7.1 %fusion.266 = (f32[1,128,1280]{2,1,0:T(8,128)}, f32[1,128,1280]{2,1,0:T(8,128)S(1)}, f32[1,128,1280]{2,1,0:T(8,128)S(1)}, f32[1,128,1280]{2,1,0:T(8,128)S(1)}, f...) fusion(f32[16,128,1280]{2,1,0:T(8,128)} %all-gather.14.cloned.1, ...), kind=kLoop, calls=%fused_computation.594 | loop fusion | bytes 20971520 | tf_op jit(solution)/shard_map/slice | solution.py:36
  392.9 2.2 copy.192
  410.4 5.0 fusion.33
  417.8 22.1 %all-gather.6 = f32[2048,20]{0,1:T(8,128)S(1)} all-gather(f32[128,20]{0,1:T(8,128)} %get-tuple-element.39), channel_id=8, replica_groups=mesh['grp'=2,'seq_0'=16,'seq_1'=4,'seq_2'=2] {'seq_0'}, dimensions={0}, use_global_device_ids=true | all-gather | bytes 174080 | tf_op jit(solution)/shard_map/all_gather | solution.py:35
  440.5 11.0 %all_gather.118 = f32[4,128,20]{1,2,0:T(8,128)S(1)} all-gather(f32[1,128,20]{1,2,0:T(8,128)S(1)} %get-tuple-element.38), channel_id=1, replica_groups=mesh['grp'=2,'seq_0'=16,'seq_1'=4,'seq_2'=2] {'seq_1'}, dimensions={0}, use_global_device_ids=true | all-gather | bytes 51200 | tf_op jit(solution)/shard_map/all_gather | solution.py:35
  458.0 22.3 %all-gather.4 = f32[2048,20]{0,1:T(8,128)S(1)} all-gather(f32[128,20]{0,1:T(8,128)S(1)} %bitcast.1448), channel_id=6, replica_groups=mesh['grp'=2,'seq_0'=16,'seq_1'=4,'seq_2'=2] {'seq_0'}, dimensions={0}, use_global_device_ids=true | all-gather | bytes 174080 | tf_op jit(solution)/shard_map/all_gather | solution.py:35
  480.3 10.7 %all_gather.123 = f32[4,128,20]{1,2,0:T(8,128)} all-gather(f32[1,128,20]{1,2,0:T(8,128)} %get-tuple-element.37), channel_id=1, replica_groups=mesh['grp'=2,'seq_0'=16,'seq_1'=4,'seq_2'=2] {'seq_1'}, dimensions={0}, use_global_device_ids=true | all-gather | bytes 51200 | tf_op jit(solution)/shard_map/all_gather | solution.py:35
  491.1 9.1 %all_gather.107 = f32[4,128,20]{1,2,0:T(8,128)S(1)} all-gather(f32[1,128,20]{1,2,0:T(8,128)S(1)} %get-tuple-element.15), channel_id=1, replica_groups=mesh['grp'=2,'seq_0'=16,'seq_1'=4,'seq_2'=2] {'seq_1'}, dimensions={0}, use_global_device_ids=true | all-gather | bytes 51200 | tf_op jit(solution)/shard_map/all_gather | solution.py:35
  504.5 23.2 %all_gather.124 = f32[2,128,20]{1,2,0:T(8,128)S(1)} all-gather(f32[1,128,20]{1,2,0:T(8,128)S(1)} %get-tuple-element.35), channel_id=1, replica_groups=mesh['grp'=2,'seq_0'=16,'seq_1'=4,'seq_2'=2] {'seq_2'}, dimensions={0}, use_global_device_ids=true | all-gather | bytes 30720 | tf_op jit(solution)/shard_map/all_gather | solution.py:35
  529.6 9.0 %all_gather.112 = f32[4,128,20]{1,2,0:T(8,128)S(1)} all-gather(f32[1,128,20]{1,2,0:T(8,128)S(1)} %get-tuple-element.14), channel_id=1, replica_groups=mesh['grp'=2,'seq_0'=16,'seq_1'=4,'seq_2'=2] {'seq_1'}, dimensions={0}, use_global_device_ids=true | all-gather | bytes 51200 | tf_op jit(solution)/shard_map/all_gather | solution.py:35
  538.7 4.8 all_gather.113
  545.4 2.7 fusion.272
  552.4 2.5 fusion.271
  (154 shorter events, 116.9 us)
Async XLA Ops:
  6.5 1.9 copy-start
  6.6 244.0 %all-gather.20.cloned.1.call-start = ((), (), s32[]{:S(2)}) async-start(), calls=%async_computation.3 | async-start | bytes 11141120 | tf_op jit(solution)/shard_map/all_gather | solution.py:35
  19.3 5.7 %copy-start.13 = (s32[2,128]{1,0:T(2,128)S(1)}, s32[2,128]{1,0:T(2,128)}, u32[]{:S(2)}) copy-start(s32[2,128]{1,0:T(2,128)} %param.14) | copy-start | bytes 3076
  19.3 7.0 %copy-start.12 = (bf16[1280,10]{0,1:T(8,128)(2,1)S(1)}, bf16[1280,10]{0,1:T(8,128)(2,1)}, u32[]{:S(2)}) copy-start(bf16[1280,10]{0,1:T(8,128)(2,1)} %param.10) | copy-start | bytes 76804
  108.8 6.1 %copy-start.14 = (f32[20]{0:T(128)S(1)}, f32[20]{0:T(128)}, u32[]{:S(2)}) copy-start(f32[20]{0:T(128)} %param.13) | copy-start | bytes 244
  112.2 2.8 copy-start.7
  112.2 2.8 copy-start.8
  115.0 3.6 copy-start.3
  115.0 3.6 copy-start.9
  121.5 4.3 copy-start.2
  121.5 4.9 copy-start.6
  131.6 245.4 %all-gather.14.cloned.1.call-start = ((), (), s32[]{:S(2)}) async-start(), calls=%async_computation | async-start | bytes 11141120 | tf_op jit(solution)/shard_map/all_gather | solution.py:35
  136.9 316.0 %all-gather.22.cloned.1.call-start = ((), (), s32[]{:S(2)}) async-start(), calls=%async_computation.4 | async-start | bytes 3276800 | tf_op jit(solution)/shard_map/all_gather | solution.py:35
  291.3 208.9 %all-gather.16.cloned.1.call-start = ((), (), s32[]{:S(2)}) async-start(), calls=%async_computation.1 | async-start | bytes 3276800 | tf_op jit(solution)/shard_map/all_gather | solution.py:35
  318.9 65.2 %copy-start.4 = (f32[2048,20]{0,1:T(8,128)}, f32[2048,20]{0,1:T(8,128)S(1)}, u32[]{:S(2)}) copy-start(f32[2048,20]{0,1:T(8,128)S(1)} %all-gather.3) | copy-start | bytes 491524
  417.7 127.7 %all-gather.24.cloned.1.call-start = ((), (), s32[]{:S(2)}) async-start(), calls=%async_computation.5 | async-start | bytes 1966080 | tf_op jit(solution)/shard_map/all_gather | solution.py:35
  454.8 36.2 %copy-start.5 = (f32[2048,20]{0,1:T(8,128)S(1)}, f32[2048,20]{0,1:T(8,128)}, u32[]{:S(2)}) copy-start(f32[2048,20]{0,1:T(8,128)} %copy-done.4) | copy-start | bytes 491524
  457.9 94.5 %all-gather.18.cloned.1.call-start = ((), (), s32[]{:S(2)}) async-start(), calls=%async_computation.2 | async-start | bytes 1966080 | tf_op jit(solution)/shard_map/all_gather | solution.py:35
  502.2 2.3 copy-start.10
  504.5 56.1 %copy-start.11 = (bf16[1280,10]{0,1:T(8,128)(2,1)S(1)}, bf16[1280,10]{0,1:T(8,128)(2,1)}, u32[]{:S(2)}) copy-start(bf16[1280,10]{0,1:T(8,128)(2,1)} %param.12) | copy-start | bytes 76804
  545.4 17.6 %copy-start.1 = (bf16[2,640,1280]{2,1,0:T(8,128)(2,1)S(1)}, bf16[2,640,1280]{2,1,0:T(8,128)(2,1)}, u32[]{:S(2)}) copy-start(bf16[2,640,1280]{2,1,0:T(8,128)(2,1)} %param.8) | copy-start | bytes 9830404
Sparse Core Ops, SparseCore 0:
  131.7 118.7 all-gather.19
  252.3 124.6 all-gather.13
  378.8 39.2 all-gather.21
  419.8 41.7 all-gather.15
  463.3 21.0 all-gather.23
  504.6 36.4 all-gather.17
where the time goes:
time: 577 us; the launch traced here: 570 us
  blocking collectives  234 us (41%)
  waiting for transfers between devices  138 us (24%)
  local copies, waits for them, and re-layouts  120 us (21%)
  other arithmetic  35.1 us (6%)
  matrix products  27.6 us (5%)
  between operations  14.5 us (3%)
    all_gather x12, blocking collectives, combined_by_axis(): pieces = jax.tree.map(lambda part: lax.all_gather(part, axis), x)  168 us
    all_gather x6, waiting for transfers between devices, combined_by_axis(): pieces = jax.tree.map(lambda part: lax.all_gather(part, axis), x)  138 us
    all_gather x3, blocking collectives, all_blocks(): tiles = lax.all_gather(tiles, axes[k])  65.7 us
    unnamed x75, local copies, waits for them, and re-layouts  63.3 us
    slice x6, local copies, waits for them, and re-layouts, combined_by_axis(): x = jax.tree.map(lambda part: part[0], pieces)  23.3 us
  transfers between devices with their start and end apart: 6, of which 2 were waited for; matrix products, arithmetic and copies ran while one was open for 20% of the time, Pallas kernels for 0%

commit v1 on v0

v1 whole, which is shorter than its diff:
```python
import functools

import jax
import jax.numpy as jnp
from jax import lax
from jax.experimental import pallas as pl
from jax.experimental.pallas import tpu as pltpu
from jax.sharding import Mesh
from jax.sharding import PartitionSpec as P

SEQ = ("z", "x", "c")
F32, BF16 = jnp.float32, jnp.bfloat16
HD = 64
CP = 16
NB = 16
COLS = 256
ROWS = 256
LOW = -1e30


def mm(a, b):
    return jnp.dot(a, b, preferred_element_type=F32)


def mm_t(a, b):
    return lax.dot_general(a, b, (((1,), (1,)), ((), ())), preferred_element_type=F32)


def iota(shape, dim):
    return lax.broadcasted_iota(jnp.int32, shape, dim)


def remote(src, dst, send, recv, device):
    return pltpu.make_async_remote_copy(
        src_ref=src,
        dst_ref=dst,
        send_sem=send,
        recv_sem=recv,
        device_id=device,
        device_id_type=pl.DeviceIdType.MESH,
    )


def near_first(n):
    order = []
    for d in range(1, n // 2 + 1):
        order.append(d)
        if n - d != d:
            order.append(n - d)
    return order


def pieces(value, count):
    parts = []
    for _ in range(count):
        part = value.astype(BF16).astype(F32)
        parts.append(part)
        value = value - part
    return parts


def stats_tile(peak, total, rows):
    at = iota((rows, peak.shape[-1]), 0)
    tile = jnp.zeros((rows, peak.shape[-1]), F32)
    for k, part in enumerate(pieces(peak, 3) + pieces(total, 2)):
        tile = jnp.where(at == k, part, tile)
    return tile


def kernel(
    sizes,
    frames, wkv, dec, wq, wo, pos, lens, slope,
    out,
    fr, wt, keys, vals, mask, grid_q, qpad, part, pair_in, xs, xr, zs, zr, ctx, wo_in, wo_all, o_out, o_in,
    fr_sem, wt_sem, qz_s, qz_r, qx_s, qx_r, qc_s, qc_r, wo_s, wo_r, pc_s, pc_r, x_s, x_r, z_s, z_r, g_s, g_r, h_s, h_r, o_s, o_r,
):
    nz, nx, nc, steps, frame_rows, tokens, width, heads, chunk = sizes
    n = nz * nx * nc
    z, x, c = lax.axis_index("z"), lax.axis_index("x"), lax.axis_index("c")
    own = (z * nx + x) * nc + c
    other = 1 - c
    near = near_first(nz)
    far = near[::-1]
    hpx = heads // nx
    pairs = heads // 2
    slots = hpx * HD
    span = zs.shape[-1]
    per_z = tokens // nz
    tall = steps * frame_rows

    loads = []
    for k in range(tall // ROWS):
        rows = pl.ds(k * ROWS, ROWS)
        loads.append(pltpu.make_async_copy(frames.at[rows, :], fr.at[rows, :], fr_sem.at[k]))
    tiles = 2 * width // COLS
    for load in loads:
        load.start()

    def tile_load(j):
        cols = pl.ds(pl.multiple_of(j * COLS, COLS), COLS)
        return pltpu.make_async_copy(wkv.at[:, cols], wt.at[:, cols], wt_sem.at[j])

    for j in range(tiles):
        tile_load(j).start()

    barrier = pltpu.get_barrier_semaphore()
    for d in far:
        pl.semaphore_signal(barrier, inc=1, device_id={"z": lax.rem(z + d, nz)}, device_id_type=pl.DeviceIdType.MESH)
    for d in range(1, nx):
        pl.semaphore_signal(barrier, inc=1, device_id={"x": lax.rem(x + d, nx)}, device_id_type=pl.DeviceIdType.MESH)
    pl.semaphore_signal(barrier, inc=1, device_id={"c": other}, device_id_type=pl.DeviceIdType.MESH)

    qpad[...] = jnp.zeros_like(qpad)
    qpad[:chunk] = mm_t(wq[...], dec[...])
    grid_q[own] = qpad[...].astype(BF16)
    grid_q[pl.ds(n, grid_q.shape[0] - n)] = jnp.zeros((grid_q.shape[0] - n, CP, grid_q.shape[2]), BF16)

    at_lane = iota((frame_rows, 128), 1)
    at_row = iota((frame_rows, 128), 0)
    for t in range(steps):
        hidden = (at_lane == 0) & (at_row >= lens[t, own])
        mask[t] = jnp.where(hidden, LOW, 0.0).astype(BF16)

    for load in loads:
        load.wait()

    def project_keys(j, carry):
        tile_load(j).wait()
        cols = pl.ds(pl.multiple_of(j * COLS, COLS), COLS)

        def rows_of(m, carry):
            rows = pl.ds(pl.multiple_of(m * ROWS, ROWS), ROWS)
            keys[rows, cols] = mm(fr[rows, :], wt[:, cols]).astype(BF16)
            return carry

        return lax.fori_loop(0, tall // ROWS, rows_of, carry)

    def project_values(j, carry):
        tile_load(j + tiles // 2).wait()
        cols = pl.ds(pl.multiple_of(j * COLS + width, COLS), COLS)
        head_rows = pl.ds(pl.multiple_of(j * COLS, COLS), COLS)

        def rows_of(m, carry):
            rows = pl.ds(pl.multiple_of(m * ROWS, ROWS), ROWS)
            vals[head_rows, rows] = mm(fr[rows, :], wt[:, cols]).T.astype(BF16)
            return carry

        return lax.fori_loop(0, tall // ROWS, rows_of, carry)

    lax.fori_loop(0, tiles // 2, project_keys, 0)

    pl.semaphore_wait(barrier, nz - 1 + nx - 1 + 1)

    def q_chunk(zz, xx, cc):
        return grid_q.at[(zz * nx + xx) * nc + cc]

    def q_over_z(k, zz):
        return remote(q_chunk(z, x, c), q_chunk(z, x, c), qz_s.at[k], qz_r.at[z], {"z": zz})

    for d in far:
        q_over_z(d, lax.rem(z + d, nz)).start()
    to_partner = remote(wo, wo_in, wo_s, wo_r, {"c": other})
    to_partner.start()

    lax.fori_loop(0, tiles // 2, project_values, 0)

    def q_over_x(zz, d):
        here = q_chunk(zz, x, c)
        return remote(here, here, qx_s.at[zz, d], qx_r.at[zz, x], {"x": lax.rem(x + d, nx)})

    def q_over_c(zz, xx):
        here = q_chunk(zz, xx, c)
        return remote(here, here, qc_s.at[zz, xx], qc_r.at[zz, xx], {"c": other})

    for d in [0] + near:
        zz = lax.rem(z + d, nz)
        if d:
            here = q_chunk(zz, x, c)
            remote(here, here, qz_s.at[d], qz_r.at[zz], {"z": zz}).wait_recv()
        for e in range(1, nx):
            q_over_x(zz, e).start()
        q_over_c(zz, x).start()
    for d in [0] + near:
        zz = lax.rem(z + d, nz)
        for e in range(1, nx):
            xx = lax.rem(x + e, nx)
            here = q_chunk(zz, xx, c)
            remote(here, here, qx_s.at[zz, e], qx_r.at[zz, xx], {"x": xx}).wait_recv()
            q_over_c(zz, xx).start()

    to_partner.wait_recv()
    wo_all[...] = jnp.zeros_like(wo_all)
    for xx in range(nx):
        for i in range(hpx):
            cols = pl.ds((i * nx + xx) * HD, HD)
            wo_all[xx, :chunk, pl.ds(i * HD, HD)] = wo[:, cols]
            wo_all[xx, CP : CP + chunk, pl.ds(i * HD, HD)] = wo_in[:, cols]

    for d in [0] + near:
        zz = lax.rem(z + d, nz)
        for xx in range(nx):
            here = q_chunk(zz, xx, other)
            remote(here, here, qc_s.at[zz, xx], qc_r.at[zz, xx], {"c": other}).wait_recv()

    place = lax.rem(own + 1, n).astype(F32)
    dist = [jnp.abs(pos[pl.ds(s, 1), :].astype(F32) - place) / n for s in range(steps)]
    ones_rows = jnp.ones((16, frame_rows), BF16)
    lane = iota((2 * HD, steps * tokens), 1)
    row = iota((2 * HD, steps * tokens), 0)
    sel_lane = iota((2 * HD, NB * CP), 1)
    sel_row = iota((2 * HD, NB * CP), 0)
    unit = jnp.where(row == 0, 1.0, 0.0).astype(BF16)

    def weigh(t, p, rhs):
        at = pl.ds(pl.multiple_of(p * 2 * HD, 2 * HD), 2 * HD)
        lhs = jnp.concatenate([keys[pl.ds(t * frame_rows, frame_rows), at], mask[t]], axis=1)
        score = mm(lhs, rhs)
        peak = jnp.max(score, axis=0, keepdims=True)
        return jnp.exp(score - peak).astype(BF16), peak

    def summed(t, p, first, count, weight):
        at = pl.ds(pl.multiple_of(p * 2 * HD + first, HD), count)
        lhs = jnp.concatenate([vals[at, pl.ds(t * frame_rows, frame_rows)], ones_rows], axis=0)
        return mm(lhs, weight)

    def store_part(s, h, context, total, peak):
        part[s, h, pl.ds(0, HD), :] = context
        eight = iota((8, tokens), 0)
        part[s, h, pl.ds(HD, 8), :] = jnp.where(eight == 0, total, peak)

    def pair_copy(p):
        two = pl.ds(2 * p, 2)
        return remote(part.at[other, two], pair_in.at[two], pc_s.at[p], pc_r.at[p], {"c": other})

    def one_pair(p, carry):
        first = (2 * HD * p) // chunk
        base = chunk * first - 2 * HD * p
        inner = sel_lane & (CP - 1)
        dim = base + chunk * (sel_lane >> 4) + inner
        pick = jnp.where((dim == sel_row) & (inner < chunk), HD**-0.5, 0.0).astype(BF16)
        q_rows = grid_q[pl.ds(first, NB)].reshape(NB * CP, steps * tokens)
        q_two = mm(pick, q_rows)
        rhs = [
            jnp.concatenate([jnp.where((row < HD) == (i == 0), q_two, 0.0).astype(BF16), unit], axis=0)
            for i in range(2)
        ]
        rhs_late = jnp.concatenate([r[:, tokens:] for r in rhs], axis=1)
        w_late, top_late = weigh(1, p, rhs_late)
        late = summed(1, p, 0, 2 * HD, w_late)
        for i in range(2):
            h = 2 * p + i
            w_old, top_old = weigh(0, p, rhs[i])
            old = summed(0, p, i * HD, HD, w_old)
            lanes = slice(i * tokens, (i + 1) * tokens)
            store_part(
                0, h, old[:HD, :tokens], old[HD : HD + 8, :tokens], top_old[:, :tokens] - slope[h] * dist[0]
            )
            peak_a = top_old[:, tokens:] - slope[h] * (dist[1] + 1.0)
            peak_b = top_late[:, lanes] - slope[h] * dist[1]
            peak = jnp.maximum(peak_a, peak_b)
            fa, fb = jnp.exp(peak_a - peak), jnp.exp(peak_b - peak)
            store_part(
                1,
                h,
                fa * old[:HD, tokens:] + fb * late[i * HD : (i + 1) * HD, lanes],
                fa * old[HD : HD + 8, tokens:] + fb * late[2 * HD : 2 * HD + 8, lanes],
                peak,
            )
        pair_copy(p).start()
        return carry

    lax.fori_loop(0, pairs, one_pair, 0)

    def x_copy(h):
        i, xx = h // nx, lax.rem(h, nx)
        return remote(xs.at[h], xr.at[x, i], x_s.at[h], x_r.at[x, i], {"x": xx})

    def merge_pair(p, carry):
        two = pl.ds(2 * p, 2)
        remote(part.at[other, two], pair_in.at[two], pc_s.at[p], pc_r.at[p], {"c": other}).wait_recv()
        for i in range(2):
            h = 2 * p + i
            mine, theirs = part[c, h], pair_in[h]
            peak_a, peak_b = mine[HD + 1 : HD + 2], theirs[HD + 1 : HD + 2]
            peak = jnp.maximum(peak_a, peak_b)
            fa, fb = jnp.exp(peak_a - peak), jnp.exp(peak_b - peak)
            merged = fa * mine[:HD] + fb * theirs[:HD]
            total = fa * mine[HD : HD + 1] + fb * theirs[HD : HD + 1]
            message = jnp.concatenate([merged, stats_tile(peak, total, 16)], axis=0).astype(BF16)

            @pl.when(lax.rem(h, nx) == x)
            def _():
                xr[x, h // nx] = message

            @pl.when(lax.rem(h, nx) != x)
            def _():
                xs[h] = message
                x_copy(h).start()

        return carry

    lax.fori_loop(0, pairs, merge_pair, 0)

    blocks, notes = [], []
    for i in range(hpx):
        for d in range(1, nx):
            xx = lax.rem(x + d, nx)
            remote(xs.at[i], xr.at[xx, i], x_s.at[i], x_r.at[xx, i], {"x": xx}).wait_recv()
        got = [xr[k, i].astype(F32) for k in range(nx)]
        peaks = [g[HD : HD + 1] + g[HD + 1 : HD + 2] + g[HD + 2 : HD + 3] for g in got]
        peak = functools.reduce(jnp.maximum, peaks)
        factors = [jnp.exp(one - peak) for one in peaks]
        blocks.append(sum(f * g[:HD] for f, g in zip(factors, got)))
        total = sum(f * (g[HD + 3 : HD + 4] + g[HD + 4 : HD + 5]) for f, g in zip(factors, got))
        notes.append(stats_tile(peak, total, 8))
    spare = span - hpx * (HD + 8)
    if spare:
        notes.append(jnp.zeros((spare, tokens), F32))
    by_token = jnp.concatenate(blocks + notes, axis=0).T
    zs[...] = by_token.reshape(nz, per_z, span).astype(BF16)
    zr[z] = zs[z]

    for d in far:
        zz = lax.rem(z + d, nz)
        remote(zs.at[zz], zr.at[z], z_s.at[d], z_r.at[z], {"z": zz}).start()
    for d in near:
        zz = lax.rem(z + d, nz)
        remote(zs.at[zz], zr.at[zz], z_s.at[d], z_r.at[zz], {"z": zz}).wait_recv()
    wide = zr[...].astype(F32)
    flat = wide.reshape(tokens, span).astype(BF16)
    from_row = iota((span, span), 0)
    to_lane = iota((span, span), 1)
    offset = from_row - slots - 8 * (to_lane >> 6)
    kept = to_lane < slots
    peak_of = jnp.where(kept & (offset >= 0) & (offset < 3), 1.0, 0.0).astype(BF16)
    total_of = jnp.where(kept & (offset >= 3) & (offset < 5), 1.0, 0.0).astype(BF16)
    peaks = mm(flat, peak_of).reshape(nz, per_z, span)
    totals = mm(flat, total_of).reshape(nz, per_z, span)
    factors = jnp.exp(peaks - jnp.max(peaks, axis=0, keepdims=True))
    context = jnp.sum(factors * wide, axis=0) / jnp.sum(factors * totals, axis=0)
    context = jnp.where(iota((per_z, span), 1) < slots, context, 0.0)
    ctx[x, z] = context.astype(BF16)

    for d in far:
        here = ctx.at[x, z]
        remote(here, here, g_s.at[d], g_r.at[z], {"z": lax.rem(z + d, nz)}).start()
    for d in [0] + near:
        zz = lax.rem(z + d, nz)
        here = ctx.at[x, zz]
        if d:
            remote(here, here, g_s.at[d], g_r.at[zz], {"z": zz}).wait_recv()
        for e in range(1, nx):
            remote(here, here, h_s.at[zz, e], h_r.at[zz, x], {"x": lax.rem(x + e, nx)}).start()
    for d in [0] + near:
        zz = lax.rem(z + d, nz)
        for e in range(1, nx):
            xx = lax.rem(x + e, nx)
            there = ctx.at[xx, zz]
            remote(there, there, h_s.at[zz, e], h_r.at[zz, xx], {"x": xx}).wait_recv()
    result = jnp.zeros((2 * CP, tokens), F32)
    for xx in range(nx):
        rows = ctx[xx].astype(F32).reshape(tokens, span).astype(BF16)
        result += mm_t(wo_all[xx], rows)
    o_out[...] = result[CP:].astype(BF16)
    swap = remote(o_out, o_in, o_s, o_r, {"c": other})
    swap.start()
    mine = result[:chunk]

    for d in near:
        zz = lax.rem(z + d, nz)
        q_over_z(d, zz).wait_send()
        remote(zs.at[zz], zr.at[z], z_s.at[d], z_r.at[z], {"z": zz}).wait_send()
        remote(ctx.at[x, z], ctx.at[x, z], g_s.at[d], g_r.at[z], {"z": zz}).wait_send()

    def close_z(zz, carry):
        for e in range(1, nx):
            q_over_x(zz, e).wait_send()
            here = ctx.at[x, zz]
            remote(here, here, h_s.at[zz, e], h_r.at[zz, x], {"x": lax.rem(x + e, nx)}).wait_send()
        for xx in range(nx):
            q_over_c(zz, xx).wait_send()
        return carry

    lax.fori_loop(0, nz, close_z, 0)

    def close_pair(p, carry):
        pair_copy(p).wait_send()
        for i in range(2):
            h = 2 * p + i

            @pl.when(lax.rem(h, nx) != x)
            def _():
                x_copy(h).wait_send()

        return carry

    lax.fori_loop(0, pairs, close_pair, 0)
    to_partner.wait_send()
    swap.wait()
    theirs = o_in[...].astype(F32)[:chunk]
    both = [jnp.where(c == 0, mine, theirs), jnp.where(c == 0, theirs, mine)]
    out[...] = jnp.stack(both, axis=1).astype(BF16)


def local(frames, dec_states, w_query, w_keyval, w_output, head_slope, lengths, positions):
    nz, nx, nc = (lax.axis_size(a) for a in SEQ)
    steps, frame_rows, width = frames.shape
    tokens = dec_states.shape[1]
    heads = head_slope.shape[0]
    chunk = w_query.shape[1]
    n = nz * nx * nc
    hpx = heads // nx
    span = -(-hpx * (HD + 8) // 128) * 128
    per_z = tokens // nz
    tall = steps * frame_rows
    sizes = (nz, nx, nc, steps, frame_rows, tokens, width, heads, chunk)
    vmem = pl.BlockSpec(memory_space=pltpu.VMEM)
    smem = pl.BlockSpec(memory_space=pltpu.SMEM)
    dma = pltpu.SemaphoreType.DMA
    flops = 2 * tall * width * 2 * width
    out = pl.pallas_call(
        functools.partial(kernel, sizes),
        out_shape=jax.ShapeDtypeStruct((chunk, steps, tokens), BF16),
        in_specs=[pl.BlockSpec(memory_space=pl.ANY)] * 2 + [vmem] * 4 + [smem] * 2,
        out_specs=vmem,
        scratch_shapes=[
            pltpu.VMEM((tall, width), BF16),
            pltpu.VMEM((width, 2 * width), BF16),
            pltpu.VMEM((tall, width), BF16),
            pltpu.VMEM((width, tall), BF16),
            pltpu.VMEM((steps, frame_rows, 128), BF16),
            pltpu.VMEM((n + NB, CP, steps * tokens), BF16),
            pltpu.VMEM((CP, steps * tokens), F32),
            pltpu.VMEM((steps, heads, HD + 8, tokens), F32),
            pltpu.VMEM((heads, HD + 8, tokens), F32),
            pltpu.VMEM((heads, HD + 16, tokens), BF16),
            pltpu.VMEM((nx, hpx, HD + 16, tokens), BF16),
            pltpu.VMEM((nz, per_z, span), BF16),
            pltpu.VMEM((nz, per_z, span), BF16),
            pltpu.VMEM((nx, nz, per_z, span), BF16),
            pltpu.VMEM((chunk, width), BF16),
            pltpu.VMEM((nx, 2 * CP, span), BF16),
            pltpu.VMEM((CP, tokens), BF16),
            pltpu.VMEM((CP, tokens), BF16),
            dma((tall // ROWS,)),
            dma((2 * width // COLS,)),
            dma((nz,)),
            dma((nz,)),
            dma((nz, nx)),
            dma((nz, nx)),
            dma((nz, nx)),
            dma((nz, nx)),
            dma,
            dma,
            dma((heads // 2,)),
            dma((heads // 2,)),
            dma((heads,)),
            dma((nx, hpx)),
            dma((nz,)),
            dma((nz,)),
            dma((nz,)),
            dma((nz,)),
            dma((nz, nx)),
            dma((nz, nx)),
            dma,
            dma,
        ],
        compiler_params=pltpu.CompilerParams(
            collective_id=0, has_side_effects=True, vmem_limit_bytes=60 * 1024 * 1024
        ),
        cost_estimate=pl.CostEstimate(flops=flops, bytes_accessed=2 * width * (tall + 2 * width), transcendentals=0),
        name="attend",
    )(frames.reshape(tall, width), w_keyval, dec_states.reshape(steps * tokens, width), w_query.T, w_output.T,
      positions, lengths, head_slope)
    return out.transpose(1, 2, 0)


def solution(mesh):
    devices = mesh.devices.reshape(mesh.shape["grp"], 16, 4, 2)
    finer = Mesh(devices, ("grp",) + SEQ)
    return jax.shard_map(
        local,
        mesh=finer,
        in_specs=(
            P("grp", SEQ, None),
            P(None, "grp", None),
            P(None, SEQ),
            P(),
            P(None, SEQ),
            P(),
            P("grp", None),
            P(None, "grp"),
        ),
        out_specs=P(None, "grp", SEQ),
        check_vma=False,
    )
```

time: 577 us -> 107 us (0.19); the launches traced: 570 us -> 107 us
  blocking collectives: 234 us -> 0 us
  waiting for transfers between devices: 138 us -> 0 us
  local copies, waits for them, and re-layouts: 120 us -> 1.29 us
  Pallas kernels: 0 us -> 106 us
  other arithmetic: 35.1 us -> 0 us
  matrix products: 27.6 us -> 0 us
  between operations: 14.5 us -> 0.01 us
    all_gather x15 -> x0, blocking collectives: 234 us -> none  [the longest x12 168 us: combined_by_axis(): pieces = jax.tree.map(lambda part: lax.all_gather(part, axis), x)]
    all_gather x6 -> x0, waiting for transfers between devices: 138 us -> none  [combined_by_axis(): pieces = jax.tree.map(lambda part: lax.all_gather(part, axis), x)]
    pallas_call x0 -> x1, Pallas kernels: none -> 106 us  [local(): pl.pallas_call(functools.partial(kernel, sizes), out_shape=jax.ShapeDtype...]
    unnamed x75 -> x1, local copies, waits for them, and re-layouts: 63.3 us -> 1.29 us
    slice x14 -> x0, local copies, waits for them, and re-layouts: 40.2 us -> none  [the longest x6 23.3 us: combined_by_axis(): x = jax.tree.map(lambda part: part[0], pieces)]
    dot_general x10 -> x0, matrix products: 27.6 us -> none  [the longest x1 10.8 us: local(): jnp.dot(frame_rows, w_keyval, preferred_element_type=jnp.float32)]
    add x12 -> x0, other arithmetic: 13.6 us -> none  [the longest x4 11.3 us: combine_parts(): rescale(context_one, scale_one, head_count)]
    exp x20 -> x0, other arithmetic: 10.2 us -> none  [the longest x16 8.3 us: combine_parts(): scale_two = jnp.exp(peak_two - row_top)]
  transfers between devices with their start and end apart: 6 -> 0, of which waited for: 2 -> 0; matrix products, arithmetic and copies ran while one was open for 20% -> 0% of each run, Pallas kernels for 0% -> 0%
where the time goes in v1:
time: 107 us
  Pallas kernels  106 us (99%)
  local copies, waits for them, and re-layouts  1.29 us (1%)
    pallas_call x1, Pallas kernels, local(): pl.pallas_call(functools.partial(kernel, sizes), out_shape=jax.ShapeDtype...  106 us

profile of v1, /device:TPU:33, one launch (start us, length us, event | category | flops | bytes accessed | tf_op | source)
XLA Modules:
  0.0 107.2 jit_solution(18463925210984890)
XLA Ops:
  0.0 105.9 %attend.1 = bf16[10,2,128]{2,1,0:T(2,128)(2,1)} custom-call(bf16[1280,1280]{1,0:T(8,128)(2,1)} %bitcast.6, bf16[1280,2560]{1,0:T(8,128)(2,1)} %wkv.1, bf16[256,1280]{1,0:T(8,128)(2,1)} %bitcast.7, bf16[10,1280]{1,0:T(8,128)(2,1)} %bitcast.8, bf16[10,1280]{1,0:T(8,128)(2,1)} %bitcast.9, s32[2,128]{1,0:T(2,128)} %pos.1, s32[2,128]{1,0:T(2,128)} %lens.1, f32[20]{0:T(128)} %slope.1), custom_call_target="tpu_custom_call" | custom-call | flops 8388608000 | bytes 9830400 | tf_op jit(solution)/shard_map/attend/pallas_call | solution.py:421
  105.9 1.3 %copy.10 = bf16[2,128,10]{1,0,2:T(2,128)(2,1)} copy(bf16[2,128,10]{1,0,2:T(2,128)(2,1)} %bitcast.5) | data formatting | bytes 10240

commit v2 on v1

v2 whole, which is shorter than its diff:
```python
import functools

import jax
import jax.numpy as jnp
from jax import lax
from jax.experimental import pallas as pl
from jax.experimental.pallas import tpu as pltpu
from jax.sharding import Mesh
from jax.sharding import PartitionSpec as P

SEQ = ("z", "x", "c")
F32, BF16 = jnp.float32, jnp.bfloat16
HD = 64
CP = 16
NB = 16
COLS = 256
LOW = -1e30


def mm(a, b):
    return jnp.dot(a, b, preferred_element_type=F32)


def mm_t(a, b):
    return lax.dot_general(a, b, (((1,), (1,)), ((), ())), preferred_element_type=F32)


def iota(shape, dim):
    return lax.broadcasted_iota(jnp.int32, shape, dim)


def remote(src, dst, send, recv, device):
    return pltpu.make_async_remote_copy(
        src_ref=src,
        dst_ref=dst,
        send_sem=send,
        recv_sem=recv,
        device_id=device,
        device_id_type=pl.DeviceIdType.MESH,
    )


def near_first(n):
    order = []
    for d in range(1, n // 2 + 1):
        order.append(d)
        if n - d != d:
            order.append(n - d)
    return order


def pieces(value, count):
    parts = []
    for _ in range(count):
        part = value.astype(BF16).astype(F32)
        parts.append(part)
        value = value - part
    return parts


def stats_tile(peak, total, rows):
    at = iota((rows, peak.shape[-1]), 0)
    tile = jnp.zeros((rows, peak.shape[-1]), F32)
    for k, part in enumerate(pieces(peak, 3) + pieces(total, 2)):
        tile = jnp.where(at == k, part, tile)
    return tile


def kernel(
    sizes,
    frames, wkv, dec, wq, wo, pos, lens, slope,
    out,
    fr, wt, dec_v, wq_v, wo_v, keys, vals, mask, grid_q, qpad, rhs_v, score_v, weight_v, part, pair_in, xs, xr, zs, zr, ctx,
    wo_rows, wo_all, fin_out, fin_in,
    fr_sem, wt_sem, in_sem, qz_s, qz_r, qx_s, qx_r, qc_s, qc_r, wo_s, wo_r, pc_s, pc_r, x_s, x_r, z_s, z_r, g_s, g_r, f_s, f_r,
):
    nz, nx, nc, steps, frame_rows, tokens, width, heads, chunk = sizes
    n = nz * nx * nc
    z, x, c = lax.axis_index("z"), lax.axis_index("x"), lax.axis_index("c")
    row_size = nx * nc
    mine = x * nc + c
    own = z * row_size + mine
    other = 1 - c
    near = near_first(nz)
    far = near[::-1]
    reach = nz // 4
    hpx = heads // nx
    pairs = heads // 2
    per_group = nx // 2
    slots = hpx * HD
    span = zs.shape[-1]
    per_z = tokens // nz
    tall = steps * frame_rows
    tiles = 2 * width // COLS
    mesh_id = pl.DeviceIdType.MESH

    def along(d):
        return lax.rem(z + d + nz, nz)

    def row_peer(r):
        t = lax.rem(mine + r, row_size)
        return t, {"x": t // nc, "c": lax.rem(t, nc)}

    barrier = pltpu.get_barrier_semaphore()
    close = [k for d in range(1, reach + 1) for k in (d, -d)]
    for d in close[::-1]:
        pl.semaphore_signal(barrier, inc=1, device_id={"z": along(d)}, device_id_type=mesh_id)
    for r in range(1, row_size):
        pl.semaphore_signal(barrier, inc=1, device_id=row_peer(r)[1], device_id_type=mesh_id)

    small = [
        pltpu.make_async_copy(src, dst, in_sem.at[k]) for k, (src, dst) in enumerate(((dec, dec_v), (wq, wq_v), (wo, wo_v)))
    ]
    loads = [
        pltpu.make_async_copy(frames.at[pl.ds(k * frame_rows, frame_rows), :], fr.at[pl.ds(k * frame_rows, frame_rows), :], fr_sem.at[k])
        for k in range(steps)
    ]

    def tile_load(j):
        cols = pl.ds(pl.multiple_of(j * COLS, COLS), COLS)
        return pltpu.make_async_copy(wkv.at[:, cols], wt.at[:, cols], wt_sem.at[j])

    for load in small + loads:
        load.start()
    tile_load(0).start()

    grid_q[pl.ds(n, NB)] = jnp.zeros((NB, CP, steps * tokens), BF16)
    qpad[...] = jnp.zeros_like(qpad)
    small[0].wait()
    small[1].wait()
    qpad[:chunk] = mm_t(wq_v[...], dec_v[...])
    grid_q[own] = qpad[...].astype(BF16)
    small[2].wait()
    wo_rows[mine] = jnp.zeros((CP, width), BF16)
    wo_rows[mine, :chunk, :] = wo_v[...]

    pl.semaphore_wait(barrier, len(close) + row_size - 1)

    def q_chunk(zz, xx, cc):
        return grid_q.at[zz * row_size + xx * nc + cc]

    def q_over_z(k, source, d):
        here = q_chunk(source, x, c)
        return remote(here, here, qz_s.at[k], qz_r.at[source], {"z": along(d)})

    def q_over_x(zz, d):
        here = q_chunk(zz, x, c)
        return remote(here, here, qx_s.at[zz, d], qx_r.at[zz, x], {"x": lax.rem(x + d, nx)})

    def q_over_c(zz, xx):
        here = q_chunk(zz, xx, c)
        return remote(here, here, qc_s.at[zz, xx], qc_r.at[zz, xx], {"c": other})

    first_stage = [(k, z, d) for k, d in enumerate(close[::-1])]
    second_stage = [(len(close) + d - 1, along(-reach), d) for d in range(reach, 0, -1)]
    second_stage += [(len(close) + reach + d - 1, along(reach), -d) for d in range(reach - 1, 0, -1)]
    for args in first_stage:
        q_over_z(*args).start()

    def wo_over_row(r):
        return remote(wo_rows.at[mine], wo_rows.at[mine], wo_s.at[r], wo_r.at[mine], row_peer(r)[1])

    def spread(zz):
        for e in range(1, nx):
            q_over_x(zz, e).start()
        q_over_c(zz, x).start()

    spread(z)

    def arrive_z(zz):
        here = q_chunk(zz, x, c)
        remote(here, here, qz_s.at[0], qz_r.at[zz], {"z": zz}).wait_recv()

    def relay():
        arrive_z(along(-reach))
        arrive_z(along(reach))
        for args in second_stage:
            q_over_z(*args).start()
        for r in range(1, row_size):
            wo_over_row(r).start()

    def spread_near():
        for d in close:
            if abs(d) < reach:
                arrive_z(along(d))
            spread(along(d))

    distant = [d for k in range(reach + 1, nz // 2 + 1) for d in ((k, -k) if 2 * k < nz else (k,))]

    def spread_far():
        for d in distant:
            arrive_z(along(d))
            spread(along(d))

    def cross(ds):
        for d in ds:
            zz = along(d)
            for e in range(1, nx):
                xx = lax.rem(x + e, nx)
                here = q_chunk(zz, xx, c)
                remote(here, here, qx_s.at[zz, e], qx_r.at[zz, xx], {"x": xx}).wait_recv()
                q_over_c(zz, xx).start()

    at_lane = iota((frame_rows, 128), 1)
    at_row = iota((frame_rows, 128), 0)
    for t in range(steps):
        hidden = (at_lane == 0) & (at_row >= lens[t, own])
        mask[t] = jnp.where(hidden, LOW, 0.0).astype(BF16)
    for load in loads:
        load.wait()
    for j in range(1, tiles):
        tile_load(j).start()

    half = tiles // 2

    def project_keys(j, carry):
        tile_load(j).wait()
        cols = pl.ds(pl.multiple_of(j * COLS, COLS), COLS)
        keys[:, cols] = mm(fr[...], wt[:, cols]).astype(BF16)

        @pl.when(j == (half - 1) // 2)
        def _():
            relay()

        @pl.when(j == half - 1)
        def _():
            spread_near()

        return carry

    def project_values(j, carry):
        tile_load(j + half).wait()
        cols = pl.ds(pl.multiple_of(j * COLS + width, COLS), COLS)
        head_rows = pl.ds(pl.multiple_of(j * COLS, COLS), COLS)
        vals[head_rows, :] = mm(fr[...], wt[:, cols]).astype(BF16).T

        @pl.when(j == half // 2 - 1 if half > 1 else j == 0)
        def _():
            spread_far()

        @pl.when(j == half - 2 if half > 1 else j == 0)
        def _():
            cross([0] + close)

        return carry

    lax.fori_loop(0, half, project_keys, 0)
    lax.fori_loop(0, half, project_values, 0)
    cross(distant)

    for r in range(1, row_size):
        t, peer = row_peer(r)
        remote(wo_rows.at[t], wo_rows.at[t], wo_s.at[r], wo_r.at[t], peer).wait_recv()
    lane = iota((width, span), 1)
    source = ((lane >> 6) * nx + x) * HD + (lane & (HD - 1))
    take = jnp.where((iota((width, span), 0) == source) & (lane < slots), 1.0, 0.0).astype(BF16)
    wo_all[...] = mm(wo_rows[...].reshape(row_size * CP, width), take).astype(BF16)

    place = lax.rem(own + 1, n).astype(F32)
    dist = [jnp.abs(pos[pl.ds(s, 1), :].astype(F32) - place) / n for s in range(steps)]
    ones_rows = jnp.ones((16, frame_rows), BF16)
    row = iota((2 * HD, steps * tokens), 0)
    unit = jnp.where(row == 0, 1.0, 0.0).astype(BF16)
    jobs = ((0, 0), (0, 1), (1, None))
    tops = {}
    crossed = [0]

    def prepare(p):
        first = (2 * HD * p) // chunk
        while crossed[0] < min(nz, (first + NB - 1) // row_size + 1):
            for xx in range(nx):
                here = q_chunk(crossed[0], xx, other)
                remote(here, here, qc_s.at[0, 0], qc_r.at[crossed[0], xx], {"c": other}).wait_recv()
            crossed[0] += 1
        sel_lane = iota((2 * HD, NB * CP), 1)
        inner = sel_lane & (CP - 1)
        dim = chunk * first - 2 * HD * p + chunk * (sel_lane >> 4) + inner
        pick = jnp.where((dim == iota((2 * HD, NB * CP), 0)) & (inner < chunk), HD**-0.5, 0.0).astype(BF16)
        q_two = mm(pick, grid_q[pl.ds(first, NB)].reshape(NB * CP, steps * tokens))
        rhs = [
            jnp.concatenate([jnp.where((row < HD) == (i == 0), q_two, 0.0).astype(BF16), unit], axis=0)
            for i in range(2)
        ]
        rhs.append(jnp.concatenate([r[:, tokens:] for r in rhs], axis=1))
        for k in range(3):
            rhs_v[p % 2, k] = rhs[k]

    def scores(p):
        for k, (t, _) in enumerate(jobs):
            lhs = jnp.concatenate([keys[pl.ds(t * frame_rows, frame_rows), pl.ds(p * 2 * HD, 2 * HD)], mask[t]], axis=1)
            score = mm(lhs, rhs_v[p % 2, k])
            score_v[p % 2, k] = score
            tops[p, k] = jnp.max(score, axis=0, keepdims=True)

    def weights(p):
        for k in range(3):
            weight_v[p % 2, k] = jnp.exp(score_v[p % 2, k] - tops[p, k]).astype(BF16)

    def store_part(s, h, context, total, peak):
        part[s, h, pl.ds(0, HD), :] = context
        part[s, h, pl.ds(HD, 8), :] = jnp.where(iota((8, tokens), 0) == 0, total, peak)

    def sums(p):
        result = []
        for k, (t, i) in enumerate(jobs):
            at = pl.ds(p * 2 * HD + (i or 0) * HD, 2 * HD if i is None else HD)
            lhs = jnp.concatenate([vals[at, pl.ds(t * frame_rows, frame_rows)], ones_rows], axis=0)
            result.append(mm(lhs, weight_v[p % 2, k]))
        late = result[2]
        for i in range(2):
            h = 2 * p + i
            old, top_old = result[i], tops[p, i]
            lanes = slice(i * tokens, (i + 1) * tokens)
            store_part(0, h, old[:HD, :tokens], old[HD : HD + 8, :tokens], top_old[:, :tokens] - slope[h] * dist[0])
            peak_a = top_old[:, tokens:] - slope[h] * (dist[1] + 1.0)
            peak_b = tops[p, 2][:, lanes] - slope[h] * dist[1]
            peak = jnp.maximum(peak_a, peak_b)
            fa, fb = jnp.exp(peak_a - peak), jnp.exp(peak_b - peak)
            store_part(
                1,
                h,
                fa * old[:HD, tokens:] + fb * late[i * HD : (i + 1) * HD, lanes],
                fa * old[HD : HD + 8, tokens:] + fb * late[2 * HD : 2 * HD + 8, lanes],
                peak,
            )

    def pair_copy(p):
        two = pl.ds(2 * p, 2)
        return remote(part.at[other, two], pair_in.at[two], pc_s.at[p], pc_r.at[p], {"c": other})

    def x_copy(i, e):
        xx = lax.rem(x + e, nx)
        return remote(xs.at[i * nx + xx], xr.at[i, x], x_s.at[i, e], x_r.at[i, x], {"x": xx})

    def merge_group(i):
        for p in range(i * per_group, (i + 1) * per_group):
            pair_copy(p).wait_recv()
        for h in range(i * nx, (i + 1) * nx):
            own_part, their_part = part[c, h], pair_in[h]
            peak_a, peak_b = own_part[HD + 1 : HD + 2], their_part[HD + 1 : HD + 2]
            peak = jnp.maximum(peak_a, peak_b)
            fa, fb = jnp.exp(peak_a - peak), jnp.exp(peak_b - peak)
            merged = fa * own_part[:HD] + fb * their_part[:HD]
            total = fa * own_part[HD : HD + 1] + fb * their_part[HD : HD + 1]
            xs[h] = jnp.concatenate([merged, stats_tile(peak, total, 16)], axis=0).astype(BF16)
        for e in range(1, nx):
            x_copy(i, e).start()

    blocks, notes = {}, {}

    def gather_group(i):
        got = [xs[i * nx + x].astype(F32)]
        for e in range(1, nx):
            xx = lax.rem(x + e, nx)
            remote(xs.at[i], xr.at[i, xx], x_s.at[i, e], x_r.at[i, xx], {"x": xx}).wait_recv()
        for e in range(1, nx):
            got.append(xr[i, lax.rem(x + e, nx)].astype(F32))
        peaks = [g[HD : HD + 1] + g[HD + 1 : HD + 2] + g[HD + 2 : HD + 3] for g in got]
        peak = functools.reduce(jnp.maximum, peaks)
        factors = [jnp.exp(one - peak) for one in peaks]
        blocks[i] = sum(f * g[:HD] for f, g in zip(factors, got))
        total = sum(f * (g[HD + 3 : HD + 4] + g[HD + 4 : HD + 5]) for f, g in zip(factors, got))
        notes[i] = stats_tile(peak, total, 8)

    merged = gathered = 0
    for it in range(pairs + 3):
        if it < pairs:
            prepare(it)
        if 0 <= it - 1 < pairs:
            scores(it - 1)
        if 0 <= it - 2 < pairs:
            weights(it - 2)
        if 0 <= it - 3 < pairs:
            sums(it - 3)
            pair_copy(it - 3).start()
        if merged < hpx and it - 3 >= (merged + 1) * per_group - 1 + 2:
            merge_group(merged)
            merged += 1
    while merged < hpx:
        merge_group(merged)
        merged += 1
    while gathered < hpx:
        gather_group(gathered)
        gathered += 1
    filled = [blocks[i] for i in range(hpx)] + [notes[i] for i in range(hpx)]
    spare = span - hpx * (HD + 8)
    if spare:
        filled.append(jnp.zeros((spare, tokens), F32))
    by_token = jnp.concatenate(filled, axis=0).T
    zs[...] = by_token.reshape(nz, per_z, span).astype(BF16)
    zr[z] = zs[z]

    def z_copy(d):
        zz = along(d)
        return remote(zs.at[zz], zr.at[z], z_s.at[d], z_r.at[z], {"z": zz})

    for d in far:
        z_copy(d).start()
    for d in near:
        zz = along(d)
        remote(zs.at[zz], zr.at[zz], z_s.at[d], z_r.at[zz], {"z": zz}).wait_recv()
    wide = zr[...].astype(F32)
    flat = wide.reshape(tokens, span).astype(BF16)
    to_lane = iota((span, span), 1)
    offset = iota((span, span), 0) - slots - 8 * (to_lane >> 6)
    kept = to_lane < slots
    peak_of = jnp.where(kept & (offset >= 0) & (offset < 3), 1.0, 0.0).astype(BF16)
    total_of = jnp.where(kept & (offset >= 3) & (offset < 5), 1.0, 0.0).astype(BF16)
    peaks = mm(flat, peak_of).reshape(nz, per_z, span)
    totals = mm(flat, total_of).reshape(nz, per_z, span)
    factors = jnp.exp(peaks - jnp.max(peaks, axis=0, keepdims=True))
    context = jnp.sum(factors * wide, axis=0) / jnp.sum(factors * totals, axis=0)
    context = jnp.where(iota((per_z, span), 1) < slots, context, 0.0)
    ctx[z] = context.astype(BF16)

    def g_copy(d):
        return remote(ctx.at[z], ctx.at[z], g_s.at[d], g_r.at[z], {"z": along(d)})

    for d in far:
        g_copy(d).start()
    for d in near:
        zz = along(d)
        remote(ctx.at[zz], ctx.at[zz], g_s.at[d], g_r.at[zz], {"z": zz}).wait_recv()

    rows = ctx[...].astype(F32).reshape(tokens, span).astype(BF16)
    fin_out[...] = mm_t(wo_all[...], rows).reshape(row_size, CP, tokens)

    def f_copy(r):
        t, peer = row_peer(r)
        return remote(fin_out.at[t], fin_in.at[mine], f_s.at[r], f_r.at[mine], peer)

    for r in range(1, row_size):
        f_copy(r).start()
    fin_in[mine] = fin_out[mine]

    for args in first_stage + second_stage:
        q_over_z(*args).wait_send()
    for d in near:
        z_copy(d).wait_send()
        g_copy(d).wait_send()
    for r in range(1, row_size):
        wo_over_row(r).wait_send()

    def close_z(zz, carry):
        for e in range(1, nx):
            q_over_x(zz, e).wait_send()
        for xx in range(nx):
            q_over_c(zz, xx).wait_send()
        return carry

    lax.fori_loop(0, nz, close_z, 0)
    for p in range(pairs):
        pair_copy(p).wait_send()
    for i in range(hpx):
        for e in range(1, nx):
            x_copy(i, e).wait_send()
    for r in range(1, row_size):
        t, peer = row_peer(r)
        remote(fin_out.at[t], fin_in.at[t], f_s.at[r], f_r.at[t], peer).wait_recv()
    both = [sum(fin_in[xx * nc + s] for xx in range(nx))[:chunk] for s in range(steps)]
    out[...] = jnp.stack(both, axis=1).astype(BF16)
    for r in range(1, row_size):
        f_copy(r).wait_send()


def local(frames, dec_states, w_query, w_keyval, w_output, head_slope, lengths, positions):
    nz, nx, nc = (lax.axis_size(a) for a in SEQ)
    steps, frame_rows, width = frames.shape
    tokens = dec_states.shape[1]
    heads = head_slope.shape[0]
    chunk = w_query.shape[1]
    n = nz * nx * nc
    hpx = heads // nx
    span = -(-hpx * (HD + 8) // 128) * 128
    per_z = tokens // nz
    tall = steps * frame_rows
    row_size = nx * nc
    sizes = (nz, nx, nc, steps, frame_rows, tokens, width, heads, chunk)
    vmem = pl.BlockSpec(memory_space=pltpu.VMEM)
    smem = pl.BlockSpec(memory_space=pltpu.SMEM)
    dma = pltpu.SemaphoreType.DMA
    flops = 2 * tall * width * 2 * width
    out = pl.pallas_call(
        functools.partial(kernel, sizes),
        out_shape=jax.ShapeDtypeStruct((chunk, steps, tokens), BF16),
        in_specs=[pl.BlockSpec(memory_space=pl.ANY)] * 5 + [vmem] + [smem] * 2,
        out_specs=vmem,
        scratch_shapes=[
            pltpu.VMEM((tall, width), BF16),
            pltpu.VMEM((width, 2 * width), BF16),
            pltpu.VMEM((steps * tokens, width), BF16),
            pltpu.VMEM((chunk, width), BF16),
            pltpu.VMEM((chunk, width), BF16),
            pltpu.VMEM((tall, width), BF16),
            pltpu.VMEM((width, tall), BF16),
            pltpu.VMEM((steps, frame_rows, 128), BF16),
            pltpu.VMEM((n + NB, CP, steps * tokens), BF16),
            pltpu.VMEM((CP, steps * tokens), F32),
            pltpu.VMEM((2, 3, 4 * HD, steps * tokens), BF16),
            pltpu.VMEM((2, 3, frame_rows, steps * tokens), F32),
            pltpu.VMEM((2, 3, frame_rows, steps * tokens), BF16),
            pltpu.VMEM((steps, heads, HD + 8, tokens), F32),
            pltpu.VMEM((heads, HD + 8, tokens), F32),
            pltpu.VMEM((heads, HD + 16, tokens), BF16),
            pltpu.VMEM((hpx, nx, HD + 16, tokens), BF16),
            pltpu.VMEM((nz, per_z, span), BF16),
            pltpu.VMEM((nz, per_z, span), BF16),
            pltpu.VMEM((nz, per_z, span), BF16),
            pltpu.VMEM((row_size, CP, width), BF16),
            pltpu.VMEM((row_size * CP, span), BF16),
            pltpu.VMEM((row_size, CP, tokens), F32),
            pltpu.VMEM((row_size, CP, tokens), F32),
            dma((steps,)),
            dma((2 * width // COLS,)),
            dma((3,)),
            dma((nz,)),
            dma((nz,)),
            dma((nz, nx)),
            dma((nz, nx)),
            dma((nz, nx)),
            dma((nz, nx)),
            dma((row_size,)),
            dma((row_size,)),
            dma((heads // 2,)),
            dma((heads // 2,)),
            dma((hpx, nx)),
            dma((hpx, nx)),
            dma((nz,)),
            dma((nz,)),
            dma((nz,)),
            dma((nz,)),
            dma((row_size,)),
            dma((row_size,)),
        ],
        compiler_params=pltpu.CompilerParams(
            collective_id=0, has_side_effects=True, vmem_limit_bytes=60 * 1024 * 1024
        ),
        cost_estimate=pl.CostEstimate(flops=flops, bytes_accessed=2 * width * (tall + 2 * width), transcendentals=0),
        name="attend",
    )(frames.reshape(tall, width), w_keyval, dec_states.reshape(steps * tokens, width), w_query.T, w_output.T,
      positions, lengths, head_slope)
    return out.transpose(1, 2, 0)


def solution(mesh):
    devices = mesh.devices.reshape(mesh.shape["grp"], 16, 4, 2)
    finer = Mesh(devices, ("grp",) + SEQ)
    return jax.shard_map(
        local,
        mesh=finer,
        in_specs=(
            P("grp", SEQ, None),
            P(None, "grp", None),
            P(None, SEQ),
            P(),
            P(None, SEQ),
            P(),
            P("grp", None),
            P(None, "grp"),
        ),
        out_specs=P(None, "grp", SEQ),
        check_vma=False,
    )
```

time: 107 us -> 82.1 us (0.77)
  Pallas kernels: 106 us -> 80.7 us
    pallas_call x1, Pallas kernels: 106 us -> 80.7 us  [local(): pl.pallas_call(functools.partial(kernel, sizes), out_shape=jax.ShapeDtype...]
where the time goes in v2:
time: 82.1 us; the launch traced here: 82 us
  Pallas kernels  80.7 us (98%)
  local copies, waits for them, and re-layouts  1.29 us (2%)
    pallas_call x1, Pallas kernels, local(): pl.pallas_call(functools.partial(kernel, sizes), out_shape=jax.ShapeDtype...  80.7 us

profile of v2, /device:TPU:33, one launch (start us, length us, event | category | flops | bytes accessed | tf_op | source)
XLA Modules:
  0.0 82.0 jit_solution(8452032432891190543)
XLA Ops:
  0.0 80.7 %attend.1 = bf16[10,2,128]{2,1,0:T(2,128)(2,1)} custom-call(bf16[1280,1280]{1,0:T(8,128)(2,1)} %bitcast.6, bf16[1280,2560]{1,0:T(8,128)(2,1)} %wkv.1, bf16[256,1280]{1,0:T(8,128)(2,1)} %bitcast.7, bf16[10,1280]{1,0:T(8,128)(2,1)} %bitcast.8, bf16[10,1280]{1,0:T(8,128)(2,1)} %bitcast.9, s32[2,128]{1,0:T(2,128)} %pos.1, s32[2,128]{1,0:T(2,128)} %lens.1, f32[20]{0:T(128)} %slope.1), custom_call_target="tpu_custom_call" | custom-call | flops 8388608000 | bytes 9830400 | tf_op jit(solution)/shard_map/attend/pallas_call | solution.py:483
  80.7 1.3 %copy.10 = bf16[2,128,10]{1,0,2:T(2,128)(2,1)} copy(bf16[2,128,10]{1,0,2:T(2,128)(2,1)} %bitcast.5) | data formatting | bytes 10240

commit v3 on v2

v3 whole, which is shorter than its diff:
```python
import functools

import jax
import jax.numpy as jnp
from jax import lax
from jax.experimental import pallas as pl
from jax.experimental.pallas import tpu as pltpu
from jax.sharding import Mesh
from jax.sharding import PartitionSpec as P

SEQ = ("z", "x", "c")
F32, BF16 = jnp.float32, jnp.bfloat16
HD = 64
CP = 16
COLS = 256
LOW = -1e30


def mm(a, b):
    return jnp.dot(a, b, preferred_element_type=F32)


def mm_t(a, b):
    return lax.dot_general(a, b, (((1,), (1,)), ((), ())), preferred_element_type=F32)


def iota(shape, dim):
    return lax.broadcasted_iota(jnp.int32, shape, dim)


def remote(src, dst, send, recv, device):
    return pltpu.make_async_remote_copy(
        src_ref=src,
        dst_ref=dst,
        send_sem=send,
        recv_sem=recv,
        device_id=device,
        device_id_type=pl.DeviceIdType.MESH,
    )


def near_first(n):
    order = []
    for d in range(1, n // 2 + 1):
        order.append(d)
        if n - d != d:
            order.append(n - d)
    return order


def pieces(value, count):
    parts = []
    for _ in range(count):
        part = value.astype(BF16).astype(F32)
        parts.append(part)
        value = value - part
    return parts


def log2(k):
    assert k & (k - 1) == 0
    return k.bit_length() - 1


def window(p, chunk, row_size):
    return 2 * HD * p // chunk // row_size, (2 * HD * (p + 1) - 1) // chunk // row_size + 1


def z_stages(hpx):
    return [tuple(range(hpx))]


def stage_span(stage):
    return -(-len(stage) * (HD + 8) // 128) * 128


def stats_tile(peak, total, rows):
    at = iota((rows, peak.shape[-1]), 0)
    tile = jnp.zeros((rows, peak.shape[-1]), F32)
    for k, part in enumerate(pieces(peak, 3) + pieces(total, 2)):
        tile = jnp.where(at == k, part, tile)
    return tile


def kernel(
    sizes,
    frames, wkv, dec, wq, wo, pos, lens, slope,
    out,
    *scratch,
):
    nz, nx, nc, steps, frame_rows, tokens, width, heads, chunk = sizes
    n = nz * nx * nc
    z, x, c = lax.axis_index("z"), lax.axis_index("x"), lax.axis_index("c")
    row_size = nx * nc
    mine = x * nc + c
    own = z * row_size + mine
    other = 1 - c
    near = near_first(nz)
    far = near[::-1]
    reach = nz // 4
    hpx = heads // nx
    pairs = heads // 2
    per_group = nx // 2
    stages = z_stages(hpx)
    ns = len(stages)
    it_ = iter(scratch)
    fr, wt, dec_v, wq_v, wo_v, keys, vals, mask, grid_q, qpad, rhs_v, score_v, weight_v, part, pair_in, xs, xr, wo_rows, fin_out, fin_in = (
        next(it_) for _ in range(20)
    )
    zs, zr, ctx, wo_all = ([next(it_) for _ in stages] for _ in range(4))
    fr_sem, wt_sem, in_sem, qz_s, qz_r, qx_s, qx_r, qc_s, qc_r, wo_s, wo_r, pc_s, pc_r, x_s, x_r, z_s, z_r, g_s, g_r, f_s, f_r = it_
    per_z = tokens // nz
    tall = steps * frame_rows
    tiles = 2 * width // COLS
    mesh_id = pl.DeviceIdType.MESH

    def along(d):
        return lax.rem(z + d + nz, nz)

    def slot(zz, xx, cc):
        return (zz * nc + cc) * nx + xx

    def wait_all(ref, send=None, recv=None):
        if send is not None:
            remote(ref, ref, send, send, {"c": 1 - c}).wait_send()
        else:
            remote(ref, ref, recv, recv, {"c": 1 - c}).wait_recv()

    def row_peer(r):
        t = lax.rem(mine + r, row_size)
        return t, {"x": t // nc, "c": lax.rem(t, nc)}

    small = [
        pltpu.make_async_copy(src, dst, in_sem.at[k]) for k, (src, dst) in enumerate(((dec, dec_v), (wq, wq_v), (wo, wo_v)))
    ]
    loads = [
        pltpu.make_async_copy(frames.at[pl.ds(k * frame_rows, frame_rows), :], fr.at[pl.ds(k * frame_rows, frame_rows), :], fr_sem.at[k])
        for k in range(steps)
    ]

    def tile_load(j):
        cols = pl.ds(pl.multiple_of(j * COLS, COLS), COLS)
        return pltpu.make_async_copy(wkv.at[:, cols], wt.at[:, cols], wt_sem.at[j])

    for load in small + loads:
        load.start()
    tile_load(0).start()

    barrier = pltpu.get_barrier_semaphore()
    close = [k for d in range(1, reach + 1) for k in (d, -d)]
    for d in close[::-1]:
        pl.semaphore_signal(barrier, inc=1, device_id={"z": along(d)}, device_id_type=mesh_id)
    for r in range(1, row_size):
        pl.semaphore_signal(barrier, inc=1, device_id=row_peer(r)[1], device_id_type=mesh_id)

    qpad[...] = jnp.zeros_like(qpad)
    small[0].wait()
    small[1].wait()
    qpad[:chunk] = mm_t(wq_v[...], dec_v[...])
    grid_q[slot(z, x, c)] = qpad[...].astype(BF16)
    pl.semaphore_wait(barrier, len(close) + row_size - 1)

    def q_chunk(zz, xx, cc):
        return grid_q.at[slot(zz, xx, cc)]

    def q_over_z(source, d):
        here = q_chunk(source, x, c)
        return remote(here, here, qz_s, qz_r.at[source], {"z": along(d)})

    def q_over_x(zz, d):
        here = q_chunk(zz, x, c)
        return remote(here, here, qx_s, qx_r.at[zz], {"x": lax.rem(x + d, nx)})

    def q_over_c(zz, cc):
        here = grid_q.at[pl.ds(slot(zz, 0, cc), nx)]
        return remote(here, here, qc_s, qc_r.at[zz], {"c": other})

    first_stage = [(z, d) for d in close[::-1]]
    second_stage = [(along(-reach), d) for d in range(reach, 0, -1)]
    second_stage += [(along(reach), -d) for d in range(reach - 1, 0, -1)]
    for args in first_stage:
        q_over_z(*args).start()

    def wo_over_row(r):
        return remote(wo_rows.at[mine], wo_rows.at[mine], wo_s, wo_r, row_peer(r)[1])

    def spread(zz):
        for e in range(1, nx):
            q_over_x(zz, e).start()

    def arrive_z(zz):
        here = q_chunk(zz, x, c)
        wait_all(here, recv=qz_r.at[zz])

    def relay():
        arrive_z(along(-reach))
        arrive_z(along(reach))
        for args in second_stage:
            q_over_z(*args).start()
        for d in (-reach, reach):
            spread(along(d))

    def spread_near():
        for d in close:
            if abs(d) < reach:
                arrive_z(along(d))
                spread(along(d))

    distant = [*range(reach + 1, nz // 2), *range(-nz // 2 + 1, -reach), nz // 2]

    def spread_far():
        for d in distant:
            arrive_z(along(d))
            spread(along(d))

    crossed = [0, 0]

    def cross_rows(after):
        for zz in range(crossed[0], after):
            wait_all(grid_q.at[pl.ds(0, nx - 1)], recv=qx_r.at[zz])
            q_over_c(zz, c).start()
        crossed[0] = max(crossed[0], after)

    spread(z)
    small[2].wait()
    wo_rows[mine] = jnp.zeros((CP, width), BF16)
    wo_rows[mine, :chunk, :] = wo_v[...]
    for r in range(1, row_size):
        wo_over_row(r).start()

    at_lane = iota((frame_rows, 128), 1)
    at_row = iota((frame_rows, 128), 0)
    for t in range(steps):
        hidden = (at_lane == 0) & (at_row >= lens[t, own])
        mask[t] = jnp.where(hidden, LOW, 0.0).astype(BF16)
    loads[0].wait()
    tile_load(0).wait()
    for j in range(1, tiles):
        tile_load(j).start()

    for t in range(steps):
        if t:
            loads[t].wait()
        rows = pl.ds(t * frame_rows, frame_rows)
        keys[rows, :COLS] = mm(fr[rows, :], wt[:, :COLS]).astype(BF16)
    half = tiles // 2

    def project_keys(j, carry):
        tile_load(j).wait()
        cols = pl.ds(pl.multiple_of(j * COLS, COLS), COLS)
        keys[:, cols] = mm(fr[...], wt[:, cols]).astype(BF16)

        @pl.when(j == max(half // 2, 1))
        def _():
            spread_near()

        @pl.when(j == max(half - 2, 1))
        def _():
            relay()

        return carry

    def project_values(j, carry):
        tile_load(j + half).wait()
        cols = pl.ds(pl.multiple_of(j * COLS + width, COLS), COLS)
        head_rows = pl.ds(pl.multiple_of(j * COLS, COLS), COLS)
        vals[head_rows, :] = mm(fr[...], wt[:, cols]).astype(BF16).T

        @pl.when(j == min(half // 2 - 1, half - 2))
        def _():
            spread_far()

        @pl.when(j == half - 2)
        def _():
            cross_rows(window(per_group - 1, chunk, row_size)[1])

        return carry

    lax.fori_loop(1, half, project_keys, 0)
    lax.fori_loop(0, half, project_values, 0)

    place = lax.rem(own + 1, n).astype(F32)
    dist = [jnp.abs(pos[pl.ds(s, 1), :].astype(F32) - place) / n for s in range(steps)]
    ones_rows = jnp.ones((16, frame_rows), BF16)
    row = iota((2 * HD, steps * tokens), 0)
    unit = jnp.where(row == 0, 1.0, 0.0).astype(BF16)
    jobs = ((0, 0), (0, 1), (1, None))
    tops = {}
    def prepare(p):
        first, after = window(p, chunk, row_size)
        if p % per_group == 0:
            cross_rows(window(min(p + 2 * per_group, pairs) - 1, chunk, row_size)[1])
            last = window(p + per_group - 1, chunk, row_size)[1]
            for zz in range(crossed[1], last):
                wait_all(grid_q.at[pl.ds(0, nx)], recv=qc_r.at[zz])
            crossed[1] = max(crossed[1], last)
        depth = (after - first) * row_size * CP
        at = iota((1, depth), 1)
        inner = at & (CP - 1)
        number = at >> log2(CP)
        in_row = ((number & (nx - 1)) << log2(nc)) + ((number >> log2(nx)) & (nc - 1))
        device = first * row_size + (number & -row_size) + in_row
        dim = jnp.where(inner < chunk, chunk * device + inner - 2 * HD * p, -1)
        pick = jnp.where(iota((2 * HD, depth), 0) == dim, HD**-0.5, 0.0).astype(BF16)
        q_two = mm(pick, grid_q[pl.ds(first * row_size, depth // CP)].reshape(depth, steps * tokens))
        rhs = [
            jnp.concatenate([jnp.where((row < HD) == (i == 0), q_two, 0.0).astype(BF16), unit], axis=0)
            for i in range(2)
        ]
        rhs.append(jnp.concatenate([r[:, tokens:] for r in rhs], axis=1))
        for k in range(3):
            rhs_v[p % 2, k] = rhs[k]

    def scores(p):
        for k, (t, _) in enumerate(jobs):
            lhs = jnp.concatenate([keys[pl.ds(t * frame_rows, frame_rows), pl.ds(p * 2 * HD, 2 * HD)], mask[t]], axis=1)
            score = mm(lhs, rhs_v[p % 2, k])
            score_v[p % 2, k] = score
            tops[p, k] = jnp.max(score, axis=0, keepdims=True)

    def weights(p):
        for k in range(3):
            weight_v[p % 2, k] = jnp.exp(score_v[p % 2, k] - tops[p, k]).astype(BF16)

    def store_part(s, h, context, total, peak):
        part[s, h, pl.ds(0, HD), :] = context
        part[s, h, pl.ds(HD, 8), :] = jnp.where(iota((8, tokens), 0) == 0, total, peak)

    def sums(p):
        result = []
        for k, (t, i) in enumerate(jobs):
            at = pl.ds(p * 2 * HD + (i or 0) * HD, 2 * HD if i is None else HD)
            lhs = jnp.concatenate([vals[at, pl.ds(t * frame_rows, frame_rows)], ones_rows], axis=0)
            result.append(mm(lhs, weight_v[p % 2, k]))
        late = result[2]
        for i in range(2):
            h = 2 * p + i
            old, top_old = result[i], tops[p, i]
            lanes = slice(i * tokens, (i + 1) * tokens)
            store_part(0, h, old[:HD, :tokens], old[HD : HD + 8, :tokens], top_old[:, :tokens] - slope[h] * dist[0])
            peak_a = top_old[:, tokens:] - slope[h] * (dist[1] + 1.0)
            peak_b = tops[p, 2][:, lanes] - slope[h] * dist[1]
            peak = jnp.maximum(peak_a, peak_b)
            fa, fb = jnp.exp(peak_a - peak), jnp.exp(peak_b - peak)
            store_part(
                1,
                h,
                fa * old[:HD, tokens:] + fb * late[i * HD : (i + 1) * HD, lanes],
                fa * old[HD : HD + 8, tokens:] + fb * late[2 * HD : 2 * HD + 8, lanes],
                peak,
            )

    def core_copy(i):
        some = pl.ds(i * nx, nx)
        return remote(part.at[other, some], pair_in.at[some], pc_s, pc_r.at[i], {"c": other})

    def x_copy(i, e):
        xx = lax.rem(x + e, nx)
        return remote(xs.at[i * nx + xx], xr.at[i, x], x_s, x_r.at[i], {"x": xx})

    def merge_group(i):
        wait_all(pair_in.at[pl.ds(0, nx)], recv=pc_r.at[i])
        for h in range(i * nx, (i + 1) * nx):
            own_part, their_part = part[c, h], pair_in[h]
            peak_a, peak_b = own_part[HD + 1 : HD + 2], their_part[HD + 1 : HD + 2]
            peak = jnp.maximum(peak_a, peak_b)
            fa, fb = jnp.exp(peak_a - peak), jnp.exp(peak_b - peak)
            merged = fa * own_part[:HD] + fb * their_part[:HD]
            total = fa * own_part[HD : HD + 1] + fb * their_part[HD : HD + 1]
            xs[h] = jnp.concatenate([merged, stats_tile(peak, total, 16)], axis=0).astype(BF16)
        for e in range(1, nx):
            x_copy(i, e).start()

    blocks, notes = {}, {}

    def gather_group(i):
        got = [xs[i * nx + x].astype(F32)]
        wait_all(xr.at[i, pl.ds(0, nx - 1)], recv=x_r.at[i])
        for e in range(1, nx):
            got.append(xr[i, lax.rem(x + e, nx)].astype(F32))
        peaks = [g[HD : HD + 1] + g[HD + 1 : HD + 2] + g[HD + 2 : HD + 3] for g in got]
        peak = functools.reduce(jnp.maximum, peaks)
        factors = [jnp.exp(one - peak) for one in peaks]
        blocks[i] = sum(f * g[:HD] for f, g in zip(factors, got))
        total = sum(f * (g[HD + 3 : HD + 4] + g[HD + 4 : HD + 5]) for f, g in zip(factors, got))
        notes[i] = stats_tile(peak, total, 8)

    gathered = 0
    for it in range(pairs + 3):
        if it < pairs:
            prepare(it)
        if 0 <= it - 1 < pairs:
            scores(it - 1)
        if 0 <= it - 2 < pairs:
            weights(it - 2)
        if 0 <= it - 3 < pairs:
            sums(it - 3)
            done, left = divmod(it - 2, per_group)
            if left == 0:
                core_copy(done - 1).start()
                if done > 1:
                    merge_group(done - 2)
    merge_group(hpx - 1)

    def z_copy(k, d):
        zz = along(d)
        return remote(zs[k].at[zz], zr[k].at[z], z_s.at[k], z_r.at[k], {"z": zz})

    def z_send(k):
        stage, span = stages[k], stage_span(stages[k])
        filled = [blocks[i] for i in stage] + [notes[i] for i in stage]
        spare = span - len(stage) * (HD + 8)
        if spare:
            filled.append(jnp.zeros((spare, tokens), F32))
        by_token = jnp.concatenate(filled, axis=0).T
        zs[k][...] = by_token.reshape(nz, per_z, span).astype(BF16)
        for d in far:
            z_copy(k, d).start()
        zr[k][z] = zs[k][z]

    def g_copy(k, d):
        return remote(ctx[k].at[z], ctx[k].at[z], g_s.at[k], g_r.at[k], {"z": along(d)})

    def z_merge(k):
        span, slots = stage_span(stages[k]), len(stages[k]) * HD
        wait_all(zr[k].at[pl.ds(0, nz - 1)], recv=z_r.at[k])
        wide = zr[k][...].astype(F32)
        flat = wide.reshape(tokens, span).astype(BF16)
        to_lane = iota((1, span), 1)
        offset = iota((span, span), 0) - slots - 8 * (to_lane >> log2(HD))
        kept = to_lane < slots
        peak_of = jnp.where(kept & (offset >= 0) & (offset < 3), 1.0, 0.0).astype(BF16)
        total_of = jnp.where(kept & (offset >= 3) & (offset < 5), 1.0, 0.0).astype(BF16)
        peaks = mm(flat, peak_of).reshape(nz, per_z, span)
        totals = mm(flat, total_of).reshape(nz, per_z, span)
        factors = jnp.exp(peaks - jnp.max(peaks, axis=0, keepdims=True))
        context = jnp.sum(factors * wide, axis=0) / jnp.sum(factors * totals, axis=0)
        context = jnp.where(iota((per_z, span), 1) < slots, context, 0.0)
        ctx[k][z] = context.astype(BF16)
        for d in far:
            g_copy(k, d).start()

    for k, stage in enumerate(stages):
        while gathered <= stage[-1]:
            gather_group(gathered)
            gathered += 1
        z_send(k)

    wait_all(wo_rows.at[pl.ds(0, row_size - 1)], recv=wo_r)
    weights_in = wo_rows[...].reshape(row_size * CP, width)
    for k, stage in enumerate(stages):
        span, slots = stage_span(stage), len(stage) * HD
        lane = iota((1, span), 1)
        source = ((stage[0] + (lane >> log2(HD))) * nx + x) * HD + (lane & (HD - 1))
        source = jnp.where(lane < slots, source, -1)
        take = jnp.where(iota((width, span), 0) == source, 1.0, 0.0).astype(BF16)
        wo_all[k][...] = mm(weights_in, take).astype(BF16)

    for k in range(ns):
        z_merge(k)

    shares = jnp.zeros((row_size * CP, tokens), F32)
    for k in range(ns):
        wait_all(ctx[k].at[pl.ds(0, nz - 1)], recv=g_r.at[k])
        rows = ctx[k][...].astype(F32).reshape(tokens, stage_span(stages[k])).astype(BF16)
        shares += mm_t(wo_all[k][...], rows)
    fin_out[...] = shares.reshape(row_size, CP, tokens)

    def f_copy(r):
        t, peer = row_peer(r)
        return remote(fin_out.at[t], fin_in.at[mine], f_s, f_r, peer)

    for r in range(1, row_size):
        f_copy(r).start()
    fin_in[mine] = fin_out[mine]

    wait_all(grid_q.at[pl.ds(0, len(first_stage + second_stage))], send=qz_s)
    wait_all(grid_q.at[pl.ds(0, nz * (nx - 1))], send=qx_s)
    wait_all(grid_q.at[pl.ds(0, nz * nx)], send=qc_s)
    wait_all(wo_rows.at[pl.ds(0, row_size - 1)], send=wo_s)
    wait_all(pair_in, send=pc_s)
    wait_all(xs.at[pl.ds(0, hpx * (nx - 1))], send=x_s)
    for k in range(ns):
        wait_all(zs[k].at[pl.ds(0, nz - 1)], send=z_s.at[k])
        wait_all(ctx[k].at[pl.ds(0, nz - 1)], send=g_s.at[k])
    wait_all(fin_in.at[pl.ds(0, row_size - 1)], recv=f_r)
    both = [sum(fin_in[xx * nc + s] for xx in range(nx))[:chunk] for s in range(steps)]
    out[...] = jnp.stack(both, axis=1).astype(BF16)
    wait_all(fin_out.at[pl.ds(0, row_size - 1)], send=f_s)


def local(frames, dec_states, w_query, w_keyval, w_output, head_slope, lengths, positions):
    nz, nx, nc = (lax.axis_size(a) for a in SEQ)
    steps, frame_rows, width = frames.shape
    tokens = dec_states.shape[1]
    heads = head_slope.shape[0]
    chunk = w_query.shape[1]
    n = nz * nx * nc
    hpx = heads // nx
    spans = [stage_span(stage) for stage in z_stages(hpx)]
    per_z = tokens // nz
    tall = steps * frame_rows
    row_size = nx * nc
    sizes = (nz, nx, nc, steps, frame_rows, tokens, width, heads, chunk)
    vmem = pl.BlockSpec(memory_space=pltpu.VMEM)
    smem = pl.BlockSpec(memory_space=pltpu.SMEM)
    dma = pltpu.SemaphoreType.DMA
    flops = 2 * tall * width * 2 * width
    out = pl.pallas_call(
        functools.partial(kernel, sizes),
        out_shape=jax.ShapeDtypeStruct((chunk, steps, tokens), BF16),
        in_specs=[pl.BlockSpec(memory_space=pl.ANY)] * 5 + [vmem] + [smem] * 2,
        out_specs=vmem,
        scratch_shapes=[
            pltpu.VMEM((tall, width), BF16),
            pltpu.VMEM((width, 2 * width), BF16),
            pltpu.VMEM((steps * tokens, width), BF16),
            pltpu.VMEM((chunk, width), BF16),
            pltpu.VMEM((chunk, width), BF16),
            pltpu.VMEM((tall, width), BF16),
            pltpu.VMEM((width, tall), BF16),
            pltpu.VMEM((steps, frame_rows, 128), BF16),
            pltpu.VMEM((n, CP, steps * tokens), BF16),
            pltpu.VMEM((CP, steps * tokens), F32),
            pltpu.VMEM((2, 3, 4 * HD, steps * tokens), BF16),
            pltpu.VMEM((2, 3, frame_rows, steps * tokens), F32),
            pltpu.VMEM((2, 3, frame_rows, steps * tokens), BF16),
            pltpu.VMEM((steps, heads, HD + 8, tokens), F32),
            pltpu.VMEM((heads, HD + 8, tokens), F32),
            pltpu.VMEM((heads, HD + 16, tokens), BF16),
            pltpu.VMEM((hpx, nx, HD + 16, tokens), BF16),
            pltpu.VMEM((row_size, CP, width), BF16),
            pltpu.VMEM((row_size, CP, tokens), F32),
            pltpu.VMEM((row_size, CP, tokens), F32),
            *[pltpu.VMEM((nz, per_z, span), BF16) for _ in range(3) for span in spans],
            *[pltpu.VMEM((row_size * CP, span), BF16) for span in spans],
            dma((steps,)),
            dma((2 * width // COLS,)),
            dma((3,)),
            dma,
            dma((nz,)),
            dma,
            dma((nz,)),
            dma,
            dma((nz,)),
            dma,
            dma,
            dma,
            dma((hpx,)),
            dma,
            dma((hpx,)),
            dma((len(spans),)),
            dma((len(spans),)),
            dma((len(spans),)),
            dma((len(spans),)),
            dma,
            dma,
        ],
        compiler_params=pltpu.CompilerParams(
            collective_id=0, has_side_effects=True, vmem_limit_bytes=60 * 1024 * 1024
        ),
        cost_estimate=pl.CostEstimate(flops=flops, bytes_accessed=2 * width * (tall + 2 * width), transcendentals=0),
        name="attend",
    )(frames.reshape(tall, width), w_keyval, dec_states.reshape(steps * tokens, width), w_query.T, w_output.T,
      positions, lengths, head_slope)
    return out.transpose(1, 2, 0)


def solution(mesh):
    devices = mesh.devices.reshape(mesh.shape["grp"], 16, 4, 2)
    finer = Mesh(devices, ("grp",) + SEQ)
    return jax.shard_map(
        local,
        mesh=finer,
        in_specs=(
            P("grp", SEQ, None),
            P(None, "grp", None),
            P(None, SEQ),
            P(),
            P(None, SEQ),
            P(),
            P("grp", None),
            P(None, "grp"),
        ),
        out_specs=P(None, "grp", SEQ),
        check_vma=False,
    )
```

time: 82.1 us -> 77.2 us (0.940)
  Pallas kernels: 80.7 us -> 75.8 us
    pallas_call x1, Pallas kernels: 80.7 us -> 75.8 us  [local(): pl.pallas_call(functools.partial(kernel, sizes), out_shape=jax.ShapeDtype...]
where the time goes in v3:
time: 77.2 us; the launch traced here: 77.1 us
  Pallas kernels  75.8 us (98%)
  local copies, waits for them, and re-layouts  1.29 us (2%)
    pallas_call x1, Pallas kernels, local(): pl.pallas_call(functools.partial(kernel, sizes), out_shape=jax.ShapeDtype...  75.8 us

profile of v3, /device:TPU:33, one launch (start us, length us, event | category | flops | bytes accessed | tf_op | source)
XLA Modules:
  0.0 77.1 jit_solution(3283517746422739490)
XLA Ops:
  0.0 75.8 %attend.1 = bf16[10,2,128]{2,1,0:T(2,128)(2,1)} custom-call(bf16[1280,1280]{1,0:T(8,128)(2,1)} %bitcast.6, bf16[1280,2560]{1,0:T(8,128)(2,1)} %wkv.1, bf16[256,1280]{1,0:T(8,128)(2,1)} %bitcast.7, bf16[10,1280]{1,0:T(8,128)(2,1)} %bitcast.8, bf16[10,1280]{1,0:T(8,128)(2,1)} %bitcast.9, s32[2,128]{1,0:T(2,128)} %pos.1, s32[2,128]{1,0:T(2,128)} %lens.1, f32[20]{0:T(128)} %slope.1), custom_call_target="tpu_custom_call" | custom-call | flops 8388608000 | bytes 9830400 | tf_op jit(solution)/shard_map/attend/pallas_call | solution.py:509
  75.8 1.3 %copy.10 = bf16[2,128,10]{1,0,2:T(2,128)(2,1)} copy(bf16[2,128,10]{1,0,2:T(2,128)(2,1)} %bitcast.5) | data formatting | bytes 10240

commit v4 on v3

--- a/solution.py
+++ b/solution.py
@@ -252,11 +252,11 @@
 
         @pl.when(j == max(half // 2, 1))
         def _():
-            spread_near()
+            relay()
 
         @pl.when(j == max(half - 2, 1))
         def _():
-            relay()
+            spread_near()
 
         return carry
 
@@ -272,7 +272,7 @@
 
         @pl.when(j == half - 2)
         def _():
-            cross_rows(window(per_group - 1, chunk, row_size)[1])
+            cross_rows(window(min(1, pairs - 1), chunk, row_size)[1])
 
         return carry
 
@@ -286,14 +286,17 @@
     unit = jnp.where(row == 0, 1.0, 0.0).astype(BF16)
     jobs = ((0, 0), (0, 1), (1, None))
     tops = {}
+    def rows_for(p):
+        return window(min(p, pairs - 1), chunk, row_size)[1]
+
+    def await_rows(last, ahead):
+        cross_rows(rows_for(ahead))
+        for zz in range(crossed[1], rows_for(last)):
+            wait_all(grid_q.at[pl.ds(0, nx)], recv=qc_r.at[zz])
+        crossed[1] = max(crossed[1], rows_for(last))
+
     def prepare(p):
         first, after = window(p, chunk, row_size)
-        if p % per_group == 0:
-            cross_rows(window(min(p + 2 * per_group, pairs) - 1, chunk, row_size)[1])
-            last = window(p + per_group - 1, chunk, row_size)[1]
-            for zz in range(crossed[1], last):
-                wait_all(grid_q.at[pl.ds(0, nx)], recv=qc_r.at[zz])
-            crossed[1] = max(crossed[1], last)
         depth = (after - first) * row_size * CP
         at = iota((1, depth), 1)
         inner = at & (CP - 1)
@@ -387,6 +390,15 @@
 
     gathered = 0
     for it in range(pairs + 3):
+        done, left = divmod(it - 3, per_group)
+        if left == 0 and done > 0:
+            core_copy(done - 1).start()
+            if done > 1:
+                merge_group(done - 2)
+        if it == 0:
+            await_rows(0, 2)
+        elif it < pairs and (it == 1 or left == 0):
+            await_rows(it + per_group - 1, it + 2 * per_group - 1)
         if it < pairs:
             prepare(it)
         if 0 <= it - 1 < pairs:
@@ -395,11 +407,8 @@
             weights(it - 2)
         if 0 <= it - 3 < pairs:
             sums(it - 3)
-            done, left = divmod(it - 2, per_group)
-            if left == 0:
-                core_copy(done - 1).start()
-                if done > 1:
-                    merge_group(done - 2)
+    core_copy(hpx - 1).start()
+    merge_group(hpx - 2)
     merge_group(hpx - 1)
 
     def z_copy(k, d):

time: 77.2 us -> 76.2 us (0.987)
  Pallas kernels: 75.8 us -> 74.8 us
    pallas_call x1, Pallas kernels: 75.8 us -> 74.8 us  [local(): pl.pallas_call(functools.partial(kernel, sizes), out_shape=jax.ShapeDtype...]
where the time goes in v4:
time: 76.2 us; the launch traced here: 76.1 us
  Pallas kernels  74.8 us (98%)
  local copies, waits for them, and re-layouts  1.29 us (2%)
    pallas_call x1, Pallas kernels, local(): pl.pallas_call(functools.partial(kernel, sizes), out_shape=jax.ShapeDtype...  74.8 us

profile of v4, /device:TPU:33, one launch (start us, length us, event | category | flops | bytes accessed | tf_op | source)
XLA Modules:
  0.0 76.1 jit_solution(17402498054009621988)
XLA Ops:
  0.0 74.8 %attend.1 = bf16[10,2,128]{2,1,0:T(2,128)(2,1)} custom-call(bf16[1280,1280]{1,0:T(8,128)(2,1)} %bitcast.6, bf16[1280,2560]{1,0:T(8,128)(2,1)} %wkv.1, bf16[256,1280]{1,0:T(8,128)(2,1)} %bitcast.7, bf16[10,1280]{1,0:T(8,128)(2,1)} %bitcast.8, bf16[10,1280]{1,0:T(8,128)(2,1)} %bitcast.9, s32[2,128]{1,0:T(2,128)} %pos.1, s32[2,128]{1,0:T(2,128)} %lens.1, f32[20]{0:T(128)} %slope.1), custom_call_target="tpu_custom_call" | custom-call | flops 8388608000 | bytes 9830400 | tf_op jit(solution)/shard_map/attend/pallas_call | solution.py:518
  74.8 1.3 %copy.10 = bf16[2,128,10]{1,0,2:T(2,128)(2,1)} copy(bf16[2,128,10]{1,0,2:T(2,128)(2,1)} %bitcast.5) | data formatting | bytes 10240

commit v5 on v4

--- a/solution.py
+++ b/solution.py
@@ -142,9 +142,8 @@
         cols = pl.ds(pl.multiple_of(j * COLS, COLS), COLS)
         return pltpu.make_async_copy(wkv.at[:, cols], wt.at[:, cols], wt_sem.at[j])
 
-    for load in small + loads:
+    for load in small[:2]:
         load.start()
-    tile_load(0).start()
 
     barrier = pltpu.get_barrier_semaphore()
     close = [k for d in range(1, reach + 1) for k in (d, -d)]
@@ -152,6 +151,9 @@
         pl.semaphore_signal(barrier, inc=1, device_id={"z": along(d)}, device_id_type=mesh_id)
     for r in range(1, row_size):
         pl.semaphore_signal(barrier, inc=1, device_id=row_peer(r)[1], device_id_type=mesh_id)
+    for load in loads + small[2:]:
+        load.start()
+    tile_load(0).start()
 
     qpad[...] = jnp.zeros_like(qpad)
     small[0].wait()
@@ -290,7 +292,7 @@
         return window(min(p, pairs - 1), chunk, row_size)[1]
 
     def await_rows(last, ahead):
-        cross_rows(rows_for(ahead))
+        cross_rows(max(rows_for(ahead), rows_for(last)))
         for zz in range(crossed[1], rows_for(last)):
             wait_all(grid_q.at[pl.ds(0, nx)], recv=qc_r.at[zz])
         crossed[1] = max(crossed[1], rows_for(last))
@@ -395,9 +397,9 @@
             core_copy(done - 1).start()
             if done > 1:
                 merge_group(done - 2)
-        if it == 0:
-            await_rows(0, 2)
-        elif it < pairs and (it == 1 or left == 0):
+        if it < min(3, pairs):
+            await_rows(it, (1, 2, 4)[it])
+        elif it < pairs and left == 0:
             await_rows(it + per_group - 1, it + 2 * per_group - 1)
         if it < pairs:
             prepare(it)

time: 76.2 us -> 76.1 us (level)
  no operation moved by 1% of the time
where the time goes in v5:
time: 76.1 us; the launch traced here: 76 us
  Pallas kernels  74.7 us (98%)
  local copies, waits for them, and re-layouts  1.29 us (2%)
    pallas_call x1, Pallas kernels, local(): pl.pallas_call(functools.partial(kernel, sizes), out_shape=jax.ShapeDtype...  74.7 us

profile of v5, /device:TPU:33, one launch (start us, length us, event | category | flops | bytes accessed | tf_op | source)
XLA Modules:
  0.0 76.0 jit_solution(9338579871600357848)
XLA Ops:
  0.0 74.7 %attend.1 = bf16[10,2,128]{2,1,0:T(2,128)(2,1)} custom-call(bf16[1280,1280]{1,0:T(8,128)(2,1)} %bitcast.6, bf16[1280,2560]{1,0:T(8,128)(2,1)} %wkv.1, bf16[256,1280]{1,0:T(8,128)(2,1)} %bitcast.7, bf16[10,1280]{1,0:T(8,128)(2,1)} %bitcast.8, bf16[10,1280]{1,0:T(8,128)(2,1)} %bitcast.9, s32[2,128]{1,0:T(2,128)} %pos.1, s32[2,128]{1,0:T(2,128)} %lens.1, f32[20]{0:T(128)} %slope.1), custom_call_target="tpu_custom_call" | custom-call | flops 8388608000 | bytes 9830400 | tf_op jit(solution)/shard_map/attend/pallas_call | solution.py:520
  74.7 1.3 %copy.10 = bf16[2,128,10]{1,0,2:T(2,128)(2,1)} copy(bf16[2,128,10]{1,0,2:T(2,128)(2,1)} %bitcast.5) | data formatting | bytes 10240
